TPU v7x, 128 devices: a whole 4x4x4 slice. The times are simulated.
128 devices in a mesh: tok: 8 (over z, core), seq: 16 (over y, x).
Axes of the slice: x: 4, y: 4, z: 4, core: 2. Of those that a mesh axis runs over, the one named last changes fastest.
Arguments:
- keys: bfloat16 [16, 2, 8192, 512], P('seq', None, 'tok'), may hold values from -6 to 6
- values: bfloat16 [16, 2, 8192, 512], P('seq', None, 'tok'), may hold values from -6 to 6
- queries: bfloat16 [16, 2, 8192, 512], P('seq', None, 'tok'), may hold values from -6 to 6
- token_rate: float32 [16, 2, 8192], P('seq', None, 'tok'), may hold values from 0.1 to 1
- valid_count: int32 [16, 2], P('seq'), may hold values from 4096 to 8192
- loss_scale: float32 [1], replicated, may hold values from 128 to 2048
- w_gate: bfloat16 [512, 512], replicated, may hold values from -0.25 to 0.25
- w_up: bfloat16 [512, 512], replicated, may hold values from -0.25 to 0.25
- w_down: bfloat16 [512, 512], replicated, may hold values from -0.25 to 0.25
- out_cotangent: bfloat16 [16, 2, 8192, 512], P('seq', None, 'tok'), may hold values from -0.0625 to 0.0625
Outputs:
- fast_out: bfloat16 [16, 2, 8192, 512], P('seq', None, 'tok')
- grad_gate: float32 [512, 512], P(None, 'tok')
- grad_up: float32 [512, 512], P(None, 'tok')
- grad_down: float32 [512, 512], P('tok')
- levels: float32 [2, 512], P(None, 'tok')
All inputs are finite; a program needn't handle non-finite values.
Results may differ from a plain program's by a relative error of at most 0.0087.
Values may be sent and summed in bfloat16 or wider, within the bound.
No kernel may reach another device: no remote copies, remote signals or barrier semaphores. Data moves between devices by JAX's collectives and lax.ppermute only.
A program may use at most 128 MiB of HBM per device.

v0:
```python
import jax
import jax.numpy as jnp
from jax import lax
from jax.sharding import PartitionSpec as P

momentum_keep = 0.9
step_rate = 3.0
tiny_value = 1e-06


def forward(inputs, gate_w, up_w):
    gate = jnp.dot(inputs, gate_w, preferred_element_type=jnp.float32)
    upper = jnp.dot(inputs, up_w, preferred_element_type=jnp.float32)
    hidden = (jax.nn.silu(gate) * upper).astype(jnp.bfloat16)
    return (gate, upper, hidden)


def backward(inputs, gate, upper, hidden, down_w, cotan):
    first = (((0,), (0,)), ((), ()))
    grad_down = lax.dot_general(hidden, cotan, first, preferred_element_type=jnp.float32)
    back = lax.dot_general(
        cotan, down_w, (((1,), (1,)), ((), ())), preferred_element_type=jnp.float32
    )
    sigma = jax.nn.sigmoid(gate)
    d_upper = (back * gate * sigma).astype(jnp.bfloat16)
    d_gate = (back * upper * sigma * (1.0 + gate * (1.0 - sigma))).astype(jnp.bfloat16)
    grad_gate = lax.dot_general(inputs, d_gate, first, preferred_element_type=jnp.float32)
    grad_up = lax.dot_general(inputs, d_upper, first, preferred_element_type=jnp.float32)
    return (grad_gate, grad_up, grad_down)


def renorm(gate_w, up_w, down_w, gate_n, up_n, down_n):
    gate_w = gate_w * (gate_n / jnp.sqrt(jnp.sum(gate_w * gate_w, axis=0) + tiny_value))
    up_w = up_w * (up_n / jnp.sqrt(jnp.sum(up_w * up_w, axis=0) + tiny_value))
    down_w = down_w * (down_n / jnp.sqrt(jnp.sum(down_w * down_w, axis=1) + tiny_value))[:, None]
    return (gate_w, up_w, down_w)


def own_units(triple, start, piece):
    return (
        lax.dynamic_slice_in_dim(triple[0], start, piece, 1),
        lax.dynamic_slice_in_dim(triple[1], start, piece, 1),
        lax.dynamic_slice_in_dim(triple[2], start, piece, 0),
    )


def per_device(
    keys, values, queries, token_rate, valid_count, loss_scale, w_gate, w_up, w_down, out_cotangent
):
    rows = keys.shape[2]
    blocks = keys.shape[1]
    width = w_gate.shape[1]
    parts = lax.axis_size("tok")
    where = lax.axis_index("tok")
    piece = width // parts
    start = where * piece
    positions = where * rows + jnp.arange(rows, dtype=jnp.int32)
    scale = loss_scale[0]
    gate_full = w_gate.astype(jnp.float32)
    up_full = w_up.astype(jnp.float32)
    down_full = w_down.astype(jnp.float32)
    gate_n = jnp.sqrt(jnp.sum(gate_full * gate_full, axis=0) + tiny_value)
    up_n = jnp.sqrt(jnp.sum(up_full * up_full, axis=0) + tiny_value)
    down_n = jnp.sqrt(jnp.sum(down_full * down_full, axis=1) + tiny_value)
    state = (gate_full, up_full, down_full)
    norms = (gate_n, up_n, down_n)
    momentum = tuple((jnp.zeros_like(entry) for entry in state))
    totals = (jnp.zeros_like(gate_full), jnp.zeros_like(up_full), jnp.zeros_like(down_full))
    current = (w_gate, w_up, w_down)
    level_list = []
    output_list = []
    for index in range(blocks):
        count = valid_count[0, index]
        mask = (positions < count).astype(jnp.float32)
        inputs = keys[0, index]
        gate, upper, hidden = forward(inputs, current[0], current[1])
        factor = -(scale * token_rate[0, index] * mask / count.astype(jnp.float32))
        cotan = (factor[:, None] * values[0, index].astype(jnp.float32)).astype(jnp.bfloat16)
        grads = backward(inputs, gate, upper, hidden, current[2], cotan)
        summed = lax.psum((grads[0], grads[1], grads[2]), "tok")
        level_piece = lax.dynamic_slice_in_dim(jnp.max(jnp.abs(summed[0]), axis=0), start, piece, 0)
        level_list.append(lax.pmax(level_piece, "seq"))
        momentum = tuple(
            (momentum_keep * held + grad / scale for held, grad in zip(momentum, summed))
        )
        stepped = tuple((entry - step_rate * held for entry, held in zip(state, momentum)))
        state = renorm(stepped[0], stepped[1], stepped[2], norms[0], norms[1], norms[2])
        rounded = tuple((entry.astype(jnp.bfloat16) for entry in state))
        current = rounded
        inputs = queries[0, index]
        gate, upper, hidden = forward(inputs, current[0], current[1])
        result = jnp.dot(hidden, current[2], preferred_element_type=jnp.float32)
        output_list.append((result * mask[:, None]).astype(jnp.bfloat16))
        outer_cot = out_cotangent[0, index] * mask[:, None].astype(jnp.bfloat16)
        partial_grads = backward(inputs, gate, upper, hidden, current[2], outer_cot)
        partial_grads = lax.psum(
            (partial_grads[0], partial_grads[1], partial_grads[2]), ("tok", "seq")
        )
        totals = tuple((held + grad for held, grad in zip(totals, partial_grads)))
    levels = jnp.stack(level_list)
    finals = own_units(totals, start, piece)
    fast_out = jnp.stack(output_list)[None]
    return (fast_out, finals[0], finals[1], finals[2], levels)


def solution(mesh):
    placed = (
        P("seq", None, "tok", None),
        P("seq", None, "tok", None),
        P("seq", None, "tok", None),
        P("seq", None, "tok"),
        P("seq", None),
        P(),
        P(),
        P(),
        P(),
        P("seq", None, "tok", None),
    )
    return jax.shard_map(
        per_device,
        mesh=mesh,
        in_specs=placed,
        out_specs=(
            P("seq", None, "tok", None),
            P(None, "tok"),
            P(None, "tok"),
            P("tok", None),
            P(None, "tok"),
        ),
        check_vma=False,
    )
```

profile of v0, /device:TPU:1, one launch (start us, length us, event | category | flops | bytes accessed | tf_op | source)
XLA Modules:
  0.0 367.0 jit_solution(4516561752722353723)
XLA Ops:
  7.2 3.5 fusion.64
  10.8 2.0 fusion.62
  15.6 2.0 fusion.101
  17.6 4.2 %fusion.72 = f32[512,512]{0,1:T(8,128)} fusion(f32[1024,512]{1,0:T(8,128)} %fusion.64, f32[1024,512]{1,0:T(8,128)S(1)} %copy-done.9, bf16[1,2,1024,512]{3,2,1,0:T(8,128)(2,1)} %param.11, f32[1024]{0:T(1024)S(1)} %divide_negate_fusion.1), kind=kOutput, calls=%fused_computation.121 | convolution fusion | flops 541589504 | bytes 6295552 | tf_op jit(solution)/shard_map/dot_general | solution.py:20
  21.9 2.3 convolution_bitcast_fusion.3
  24.2 1.8 convolution_bitcast_fusion.2
  30.2 66.8 %all-reduce.12.cloned.1.call-done = (f32[512,512]{0,1:T(8,128)}, f32[512,512]{0,1:T(8,128)}, f32[512,512]{0,1:T(8,128)}) async-done(((f32[512,512]{0,1:T(8,128)}, f32[512,512]{0,1:T(8,128)}, f32[512,512]{0,1:T(8,128)}), (f32[512,512]{0,1:T(8,128)}, f32[512,512]{0,1:T(8,128)}, f32[512,512]{0,1:T(8,128)})) %all-reduce.12.cloned.1.call-update) | async-done | bytes 3145744 | tf_op jit(solution)/shard_map/psum | solution.py:80
  97.0 2.3 fusion.38
  101.5 0.9 fusion.48
  102.4 1.8 convolution_bitcast_fusion
  104.2 0.9 fusion.50
  105.1 2.3 convolution_bitcast_fusion.1
  107.4 2.2 fusion.73
  109.6 2.6 fusion.58
  112.2 1.3 copy-done.25
  113.5 2.7 fusion.23
  116.5 3.5 fusion.75
  121.6 1.8 fusion.52
  123.4 2.3 fusion.54
  125.7 59.9 %all-reduce.10.cloned.1.call-done = (f32[512,512]{0,1:T(8,128)}, f32[512,512]{0,1:T(8,128)}, f32[512,512]{0,1:T(8,128)}) async-done(((f32[512,512]{0,1:T(8,128)}, f32[512,512]{0,1:T(8,128)}, f32[512,512]{0,1:T(8,128)}), (f32[512,512]{0,1:T(8,128)}, f32[512,512]{0,1:T(8,128)}, f32[512,512]{0,1:T(8,128)})) %all-reduce.10.cloned.1.call-update) | async-done | bytes 3145744 | tf_op jit(solution)/shard_map/psum | solution.py:80
  185.6 2.3 multiply_reduce_fusion.2
  190.9 1.0 fusion.2
  193.7 1.8 fusion.35
  195.5 2.3 fusion.36
  197.8 1.8 convolution_add_fusion
  200.4 2.9 fusion.33
  203.4 33.3 %all-reduce.1 = (f32[1,64]{1,0:T(1,128)S(1)}, f32[1,64]{1,0:T(1,128)S(1)}) all-reduce(f32[1,64]{1,0:T(1,128)S(1)} %dynamic-slice_bitcast_fusion, f32[1,64]{1,0:T(1,128)S(1)} %dynamic-slice_bitcast_fusion.1), channel_id=1, replica_groups=mesh['tok'=8,'seq'=16] {'seq'}, use_global_device_ids=true, to_apply=%region_24.25 | all-reduce | flops 128 | bytes 1024 | tf_op jit(solution)/shard_map/pmax | solution.py:82
  238.0 1.5 maximum_bitcast_fusion
  239.5 116.3 %all-reduce.8.cloned.1.call-done = (f32[512,512]{0,1:T(8,128)}, f32[512,512]{0,1:T(8,128)}, f32[512,512]{1,0:T(8,128)}) async-done(((f32[512,512]{0,1:T(8,128)}, f32[512,512]{0,1:T(8,128)}, f32[512,512]{1,0:T(8,128)}), (f32[512,512]{0,1:T(8,128)}, f32[512,512]{0,1:T(8,128)}, f32[512,512]{1,0:T(8,128)})) %all-reduce.8.cloned.1.call-update) | async-done | bytes 3145744 | tf_op jit(solution)/shard_map/psum | solution.py:96
  355.8 1.6 constant_dynamic-slice_fusion.2
  357.3 1.6 constant_dynamic-slice_fusion.1
  358.9 1.6 constant_dynamic-slice_fusion
  (93 shorter events, 16.1 us)
Async XLA Ops:
  7.2 3.6 copy-start.5
  7.2 3.6 copy-start.12
  7.2 89.8 %all-reduce.12.cloned.1.call-start = ((), (), s32[]{:S(2)}) async-start(), calls=%async_computation.2 | async-start | bytes 6291456 | tf_op jit(solution)/shard_map/psum | solution.py:80
  10.8 2.7 copy-start.23
  10.8 4.0 %copy-start.22 = (f32[1,2,1024]{2,1,0:T(2,128)S(1)}, f32[1,2,1024]{2,1,0:T(2,128)}, u32[]{:S(2)}) copy-start(f32[1,2,1024]{2,1,0:T(2,128)} %param.13) | copy-start | bytes 24580
  10.8 4.8 %copy-start.13 = (bf16[512,512]{1,0:T(8,128)(2,1)S(1)}, bf16[512,512]{1,0:T(8,128)(2,1)}, u32[]{:S(2)}) copy-start(bf16[512,512]{1,0:T(8,128)(2,1)} %param.18) | copy-start | bytes 1572868
  14.8 2.8 copy-start.9
  17.6 4.2 %copy-start.10 = (f32[1024,512]{1,0:T(8,128)S(1)}, f32[1024,512]{1,0:T(8,128)}, u32[]{:S(2)}) copy-start(f32[1024,512]{1,0:T(8,128)} %fusion.64) | copy-start | bytes 6291460
  25.9 1.3 copy-start.11
  25.9 159.6 %all-reduce.10.cloned.1.call-start = ((), (), s32[]{:S(2)}) async-start(), calls=%async_computation.1 | async-start | bytes 6291456 | tf_op jit(solution)/shard_map/psum | solution.py:80
  97.0 2.3 copy-start
  97.0 2.5 copy-start.15
  99.5 1.2 copy-start.4
  99.5 1.9 copy-start.6
  102.3 1.9 copy-start.1
  109.6 3.9 %copy-start.2 = (f32[512,512]{0,1:T(8,128)S(1)}, f32[512,512]{0,1:T(8,128)}, u32[]{:S(2)}) copy-start(f32[512,512]{0,1:T(8,128)} %get-tuple-element.22) | copy-start | bytes 3145732
  109.6 3.9 %copy-start.19 = (bf16[1,2,1024,512]{3,2,1,0:T(8,128)(2,1)S(1)}, bf16[1,2,1024,512]{3,2,1,0:T(8,128)(2,1)}, u32[]{:S(2)}) copy-start(bf16[1,2,1024,512]{3,2,1,0:T(8,128)(2,1)} %param.12) | copy-start | bytes 6291460
  112.1 1.3 copy-start.25
  116.2 239.5 %all-reduce.8.cloned.1.call-start = ((), (), s32[]{:S(2)}) async-start(), calls=%async_computation | async-start | bytes 6291456 | tf_op jit(solution)/shard_map/psum | solution.py:96
  116.5 3.5 copy-start.7
  116.5 4.3 %copy-start.26 = (f32[512,1024]{0,1:T(8,128)S(1)}, f32[512,1024]{0,1:T(8,128)}, u32[]{:S(2)}) copy-start(f32[512,1024]{0,1:T(8,128)} %copy-done.25) | copy-start | bytes 6291460
  120.0 1.6 copy-start.20
  121.6 1.8 copy-start.27
  185.6 2.3 copy-start.3
  185.6 2.3 copy-start.17
  187.9 1.2 copy-start.16
  188.4 1.7 copy-start.21
  190.9 1.6 copy-start.8
  192.5 1.2 copy-start.29
  193.7 1.8 copy-start.28
  195.5 2.3 copy-start.24
  203.3 34.7 %copy-start.18 = (bf16[1,1024,512]{2,1,0:T(8,128)(2,1)S(1)}, bf16[1,1024,512]{2,1,0:T(8,128)(2,1)}, u32[]{:S(2)}) copy-start(bf16[1,1024,512]{2,1,0:T(8,128)(2,1)} %fusion.33) | copy-start | bytes 3145732
  (1 other events, 1.0 us)
Sparse Core Ops, SparseCore 0:
  26.1 70.8 all-reduce.11
  116.4 69.1 all-reduce.9
  199.8 155.9 all-reduce.7
where the time goes:
time: 367 us
  waiting for transfers between devices  243 us (66%)
  matrix products  50.5 us (14%)
  blocking collectives  33.3 us (9%)
  between operations  16.1 us (4%)
  local copies, waits for them, and re-layouts  11.9 us (3%)
  other arithmetic  11.8 us (3%)
    psum x2, waiting for transfers between devices, per_device(): summed = lax.psum((grads[0], grads[1], grads[2]), 'tok')  127 us
    psum x1, waiting for transfers between devices, per_device(): lax.psum((partial_grads[0], partial_grads[1], partial_grads[2]), ('tok',...  116 us
    pmax x1, blocking collectives, per_device(): level_list.append(lax.pmax(level_piece, 'seq'))  33.3 us
    dot_general x4, matrix products, backward(): lax.dot_general(hidden, cotan, first, preferred_element_type=jnp.float32)  11.7 us
    dot_general x4, matrix products, backward(): lax.dot_general(inputs, d_gate, first, preferred_element_type=jnp.float32)  9.18 us
    dot_general x4, matrix products, forward(): upper = jnp.dot(inputs, up_w, preferred_element_type=jnp.float32)  8.19 us
  transfers between devices with their start and end apart: 3, of which 3 were waited for; matrix products, arithmetic and copies ran while one was open for 5% of the time, Pallas kernels for 0%

commit v1 on v0

v1 whole, which is shorter than its diff:
```python
import functools
import jax
import jax.numpy as jnp
from jax import lax
from jax.experimental import pallas as pl
from jax.experimental.pallas import tpu as pltpu
from jax.sharding import PartitionSpec as P

KEEP = 0.9
RATE = 3.0
TINY = 1e-06
BF = jnp.bfloat16
F32 = jnp.float32
NT = (((1,), (1,)), ((), ()))
TN = (((0,), (0,)), ((), ()))
VMEM_LIMIT = 56 * 1024 * 1024


def dot(a, b, dims=None):
    if dims is None:
        return jnp.dot(a, b, preferred_element_type=F32)
    return lax.dot_general(a, b, dims, preferred_element_type=F32)


def smem():
    return pl.BlockSpec(memory_space=pltpu.SMEM)


def whole(array):
    return pl.BlockSpec(array.shape, lambda i: (0,) * array.ndim)


def prep_body(where_ref, gate_ref, up_ref, down_ref, out_ref, gate_t, up_t):
    gate_t[...] = gate_ref[...].T
    up_t[...] = up_ref[...].T
    where = where_ref[0]
    z = where // 2
    core = where % 2
    width = out_ref.shape[3]
    chips = out_ref.shape[1]
    for half in range(2):
        for k in range(chips):
            owner = 2 * ((z + k) % chips) + (core + half) % 2
            rows = pl.ds(pl.multiple_of(owner * width, width), width)
            out_ref[half, k, 0] = gate_t[rows, :]
            out_ref[half, k, 1] = up_t[rows, :]
            out_ref[half, k, 2] = down_ref[rows, :]


def prep(where, w_gate, w_up, w_down, parts):
    width = w_gate.shape[1] // parts
    dim = w_gate.shape[0]
    shape = (2, parts // 2, 3, width, dim)
    return pl.pallas_call(
        prep_body,
        grid=(1,),
        in_specs=[smem(), whole(w_gate), whole(w_up), whole(w_down)],
        out_specs=pl.BlockSpec(shape, lambda i: (0,) * 5),
        out_shape=jax.ShapeDtypeStruct(shape, BF),
        scratch_shapes=[pltpu.VMEM(w_gate.shape[::-1], BF), pltpu.VMEM(w_up.shape[::-1], BF)],
        name="prep",
        compiler_params=pltpu.CompilerParams(vmem_limit_bytes=VMEM_LIMIT),
    )(where, w_gate, w_up, w_down)


def gather_rows(pieces, gu, down):
    k = 0
    rows = down.shape[0]
    for ref in pieces:
        for i in range(ref.shape[0]):
            width = ref.shape[2]
            gu[k * width : (k + 1) * width] = ref[i, 0]
            gu[rows + k * width : rows + (k + 1) * width] = ref[i, 1]
            down[k * width : (k + 1) * width] = ref[i, 2]
            k += 1


def grads_of(x, e, row, gu, down):
    rows = down.shape[0]
    ab = dot(gu[...], x, NT)
    a = ab[:rows]
    b = ab[rows:]
    r = dot(down[...], e, NT) * row
    s = 0.5 + 0.5 * jnp.tanh(0.5 * a)
    act = a * s
    hidden = (act * b * row).astype(BF)
    e_up = (r * act).astype(BF)
    e_gate = (r * b * (s + act * (1.0 - s))).astype(BF)
    return (dot(e_gate, x), dot(e_up, x), dot(hidden, e), hidden)


def mask_row(where, count, step, tile, tokens):
    base = where * tokens + step * tile
    return base + lax.broadcasted_iota(jnp.int32, (1, tile), 1) < count


def half_body(inner, block, n_pieces, has_acc, where_ref, count_ref, scale_ref, rate_ref, x_ref, e_ref, *refs):
    pieces = refs[:n_pieces]
    refs = refs[n_pieces:]
    if has_acc:
        start_ref = refs[0]
        refs = refs[1:]
    out_ref, gu, down, acc = refs
    step = pl.program_id(0)
    tile = x_ref.shape[2]
    tokens = tile * pl.num_programs(0)

    @pl.when(step == 0)
    def _():
        gather_rows(pieces, gu, down)

    count = count_ref[0, block]
    valid = mask_row(where_ref[0], count, step, tile, tokens)
    if inner:
        factor = -(scale_ref[0] / count.astype(F32))
        row = jnp.where(valid, rate_ref[0, block : block + 1, :] * factor, 0.0)
    else:
        row = jnp.where(valid, 1.0, 0.0)
    g, u, d, _ = grads_of(x_ref[0, 0], e_ref[0, 0], row, gu, down)
    g = (g, u, d)

    @pl.when(step == 0)
    def _():
        for j in range(3):
            acc[j] = (start_ref[j] + g[j]) if has_acc else g[j]

    @pl.when(step != 0)
    def _():
        for j in range(3):
            acc[j] += g[j]

    @pl.when(step == pl.num_programs(0) - 1)
    def _():
        out_ref[...] = acc[...].astype(out_ref.dtype)


def half_grads(inner, block, where, count, scale, rate, x, e, pieces, out_dtype, acc=None, tile=512):
    tokens, dim = x.shape[2:]
    n_rows = sum(p.shape[0] * p.shape[2] for p in pieces)
    shape = (3, n_rows, dim)
    steps = tokens // tile
    operands = [where, count, scale, rate, x, e, *pieces]
    spec = pl.BlockSpec((1, 1, tile, dim), lambda i: (0, block, i, 0))
    specs = [smem(), smem(), smem(), pl.BlockSpec((1, rate.shape[1], tile), lambda i: (0, 0, i)), spec, spec]
    specs += [whole(p) for p in pieces]
    if acc is not None:
        operands.append(acc)
        specs.append(whole(acc))
    return pl.pallas_call(
        functools.partial(half_body, inner, block, len(pieces), acc is not None),
        grid=(steps,),
        in_specs=specs,
        out_specs=pl.BlockSpec(shape, lambda i: (0, 0, 0)),
        out_shape=jax.ShapeDtypeStruct(shape, out_dtype),
        scratch_shapes=[
            pltpu.VMEM((2 * n_rows, dim), BF),
            pltpu.VMEM((n_rows, dim), BF),
            pltpu.VMEM(shape, F32),
        ],
        name=("inner" if inner else "outer") + str(block),
        cost_estimate=pl.CostEstimate(
            flops=12 * tokens * n_rows * dim, transcendentals=tokens * n_rows, bytes_accessed=4 * tokens * dim
        ),
        compiler_params=pltpu.CompilerParams(vmem_limit_bytes=VMEM_LIMIT),
    )(*operands)


def output_body(block, n_pieces, where_ref, count_ref, x_ref, *refs):
    pieces = refs[:n_pieces]
    out_ref, gu, down = refs[-3:]
    step = pl.program_id(0)
    tile = x_ref.shape[2]

    @pl.when(step == 0)
    def _():
        gather_rows(pieces, gu, down)

    valid = mask_row(where_ref[0], count_ref[0, block], step, tile, tile * pl.num_programs(0))
    rows = down.shape[0]
    ab = dot(gu[...], x_ref[0, 0], NT)
    a = ab[:rows]
    s = 0.5 + 0.5 * jnp.tanh(0.5 * a)
    hidden = jnp.where(valid, a * s * ab[rows:], 0.0).astype(BF)
    out_ref[0, 0] = dot(hidden, down[...], TN).astype(BF)


def output_of(block, where, count, x, pieces, base=None, tile=512):
    tokens, dim = x.shape[2:]
    n_rows = sum(p.shape[0] * p.shape[2] for p in pieces)
    spec = pl.BlockSpec((1, 1, tile, dim), lambda i: (0, block, i, 0))
    operands = [where, count, x, *pieces]
    specs = [smem(), smem(), spec] + [whole(p) for p in pieces]
    alias = {}
    if base is not None:
        alias = {len(operands): 0}
        operands.append(base)
        specs.append(pl.BlockSpec(memory_space=pl.ANY))
    return pl.pallas_call(
        functools.partial(output_body, block, len(pieces)),
        grid=(tokens // tile,),
        in_specs=specs,
        out_specs=spec,
        out_shape=jax.ShapeDtypeStruct(x.shape, BF),
        scratch_shapes=[pltpu.VMEM((2 * n_rows, dim), BF), pltpu.VMEM((n_rows, dim), BF)],
        input_output_aliases=alias,
        name="output" + str(block),
        cost_estimate=pl.CostEstimate(
            flops=6 * tokens * n_rows * dim, transcendentals=tokens * n_rows, bytes_accessed=4 * tokens * dim
        ),
        compiler_params=pltpu.CompilerParams(vmem_limit_bytes=VMEM_LIMIT),
    )(*operands)


def combine_body(own_ref, other_ref, *outs):
    width = outs[0].shape[1]
    for k, out in enumerate(outs):
        rows = slice(k * width, (k + 1) * width)
        out[...] = (own_ref[:, rows, :].astype(F32) + other_ref[:, rows, :].astype(F32)).astype(out.dtype)


def combine(own, other, chips):
    shape = (3, own.shape[1] // chips, own.shape[2])
    spec = pl.BlockSpec(shape, lambda i: (0, 0, 0))
    return pl.pallas_call(
        combine_body,
        grid=(1,),
        in_specs=[whole(own), whole(other)],
        out_specs=[spec] * chips,
        out_shape=[jax.ShapeDtypeStruct(shape, F32 if k == 0 else BF) for k in range(chips)],
        name="combine",
        compiler_params=pltpu.CompilerParams(vmem_limit_bytes=VMEM_LIMIT),
    )(own, other)


def norm_of(w):
    return jnp.sqrt(jnp.sum(w * w, axis=1, keepdims=True) + TINY)


def update_body(first, n_recv, scale_ref, own_ref, *refs):
    recv = refs[:n_recv]
    refs = refs[n_recv:]
    if first:
        start_ref, piece_ref, level_ref, state_out, momentum_out, norm_out = refs
    else:
        state_ref, momentum_ref, norm_ref, piece_ref, level_ref = refs
    scale = scale_ref[0]
    for j in range(3):
        total = own_ref[j]
        for ref in recv:
            total = total + ref[j].astype(F32)
        if j == 0:
            level = jnp.max(jnp.abs(total), axis=1, keepdims=True)
            level_ref[...] = jnp.broadcast_to(level, level_ref.shape)
        if first:
            state = start_ref[0, 0, j].astype(F32)
            norm = norm_of(state)
            moved = total / scale
        else:
            state = state_ref[j]
            norm = norm_ref[j][:, :1]
            moved = KEEP * momentum_ref[j] + total / scale
        state = state - RATE * moved
        state = state * (norm / norm_of(state))
        piece_ref[0, j] = state.astype(BF)
        if first:
            state_out[j] = state
            momentum_out[j] = moved
            norm_out[j] = jnp.broadcast_to(norm, norm_out.shape[1:])


def update(scale, own, recv, start=None, carried=None):
    first = start is not None
    operands = [scale, own, *recv]
    specs = [smem(), whole(own)] + [whole(r) for r in recv]
    if first:
        operands.append(start)
        specs.append(pl.BlockSpec((1, 1) + start.shape[2:], lambda i: (0,) * 5))
    else:
        operands += list(carried)
        specs += [whole(c) for c in carried]
    shapes = [((1,) + own.shape, BF), ((own.shape[1], 128), F32)]
    if first:
        shapes += [(own.shape, F32), (own.shape, F32), (own.shape[:2] + (128,), F32)]
    return pl.pallas_call(
        functools.partial(update_body, first, len(recv)),
        grid=(1,),
        in_specs=specs,
        out_specs=[pl.BlockSpec(s, lambda i, n=len(s): (0,) * n) for s, _ in shapes],
        out_shape=[jax.ShapeDtypeStruct(s, t) for s, t in shapes],
        name="update",
        compiler_params=pltpu.CompilerParams(vmem_limit_bytes=VMEM_LIMIT),
    )(*operands)


def per_device(
    keys, values, queries, token_rate, valid_count, loss_scale, w_gate, w_up, w_down, out_cotangent
):
    parts = lax.axis_size("tok")
    seqs = lax.axis_size("seq")
    chips = parts // 2
    where = lax.axis_index("tok").reshape(1).astype(jnp.int32)

    def z_shift(array, k):
        pairs = [(2 * z + c, 2 * ((z + k) % chips) + c) for z in range(chips) for c in range(2)]
        return lax.ppermute(array, "tok", pairs)

    def other_core(array):
        return lax.ppermute(array, "tok", [(t, t ^ 1) for t in range(parts)])

    def scatter(own, other):
        sums = combine(own, other_core(other), chips)
        return sums[0], [z_shift(sums[k], k) for k in range(1, chips)]

    def spread(piece):
        mine = [piece] + [z_shift(piece, chips - k) for k in range(1, chips)]
        return mine, [other_core(p) for p in mine]

    start = prep(where, w_gate, w_up, w_down, parts)
    halves = ([start[0]], [start[1]])
    args = (where, valid_count, loss_scale, token_rate)
    levels = []
    carried = None
    for block in range(2):
        other = half_grads(True, block, *args, keys, values, halves[1], BF)
        own = half_grads(True, block, *args, keys, values, halves[0], F32)
        own, recv = scatter(own, other)
        if block == 0:
            piece, level, *carried = update(loss_scale, own, recv, start=start)
        else:
            piece, level = update(loss_scale, own, recv, carried=carried)
        levels.append(level[:, 0])
        halves = spread(piece)
        if block == 0:
            acc = [
                half_grads(False, 0, *args, queries, out_cotangent, halves[h], F32) for h in range(2)
            ]
            fast_out = output_of(0, where, valid_count, queries, halves[0] + halves[1])
    other = half_grads(False, 1, *args, queries, out_cotangent, halves[1], BF, acc=acc[1])
    own = half_grads(False, 1, *args, queries, out_cotangent, halves[0], F32, acc=acc[0])
    fast_out = output_of(1, where, valid_count, queries, halves[0] + halves[1], base=fast_out)
    own, recv = scatter(own, other)
    total = own
    for r in recv:
        total = total + r.astype(F32)
    shape = total.shape
    rows = shape[0] * shape[1] // seqs
    total = total.astype(BF).reshape(seqs, rows, shape[2])
    total = lax.all_to_all(total, "seq", 0, 0)
    total = jnp.sum(total.astype(F32), axis=0).astype(BF)
    level = jnp.concatenate(levels)
    high = lax.reduce_precision(level, 8, 7)
    mid = lax.reduce_precision(level - high, 8, 7)
    low = level - high - mid
    line = jnp.concatenate([high.astype(BF), mid.astype(BF), low.astype(BF), jnp.zeros((shape[2] - 3 * level.shape[0],), BF)])
    sent = jnp.concatenate([total, line[None]])
    sent = jnp.broadcast_to(sent[None], (seqs,) + sent.shape)
    got = lax.all_to_all(sent, "seq", 0, 0).astype(F32)
    total = got[:, :rows].reshape(shape)
    size = level.shape[0]
    line = got[:, rows]
    level = line[:, :size] + line[:, size : 2 * size] + line[:, 2 * size : 3 * size]
    level = jnp.max(level, axis=0).reshape(2, shape[1])
    return (fast_out, total[0].T, total[1].T, total[2], level)


def solution(mesh):
    placed = (
        P("seq", None, "tok", None),
        P("seq", None, "tok", None),
        P("seq", None, "tok", None),
        P("seq", None, "tok"),
        P("seq", None),
        P(),
        P(),
        P(),
        P(),
        P("seq", None, "tok", None),
    )
    return jax.shard_map(
        per_device,
        mesh=mesh,
        in_specs=placed,
        out_specs=(
            P("seq", None, "tok", None),
            P(None, "tok"),
            P(None, "tok"),
            P("tok", None),
            P(None, "tok"),
        ),
        check_vma=False,
    )
```

time: 367 us -> 176 us (0.48)
  waiting for transfers between devices: 243 us -> 43.2 us
  Pallas kernels: 0 us -> 69.6 us
  matrix products: 50.5 us -> 0 us
  starting transfers between devices: 0.52 us -> 45.9 us
  blocking collectives: 33.3 us -> 0 us
  between operations: 16.1 us -> 1.57 us
  other arithmetic: 11.8 us -> 1.3 us
    psum x3 -> x0, waiting for transfers between devices: 243 us -> none  [the longest x2 127 us: per_device(): summed = lax.psum((grads[0], grads[1], grads[2]), 'tok')]
    pallas_call x0 -> x16, Pallas kernels: none -> 69.6 us  [the longest x8 44.5 us: half_grads(): pl.pallas_call(functools.partial(half_body, inner, block, len(pieces), ac...]
    dot_general x26 -> x0, matrix products: 50.5 us -> none  [the longest x4 11.7 us: backward(): lax.dot_general(hidden, cotan, first, preferred_element_type=jnp.float32)]
    ppermute x0 -> x26, starting transfers between devices: none -> 35.6 us  [the longest x15 18.5 us: z_shift(): return lax.ppermute(array, 'tok', pairs)]
    ppermute x0 -> x26, waiting for transfers between devices: none -> 35.6 us  [the longest x15 34.5 us: z_shift(): return lax.ppermute(array, 'tok', pairs)]
    pmax x1 -> x0, blocking collectives: 33.3 us -> none  [per_device(): level_list.append(lax.pmax(level_piece, 'seq'))]
    all_to_all x0 -> x2, starting transfers between devices: none -> 10.3 us  [the longest x1 6.75 us: per_device(): total = lax.all_to_all(total, 'seq', 0, 0)]
    all_to_all x0 -> x2, waiting for transfers between devices: none -> 7.62 us  [the longest x1 7.61 us: per_device(): total = lax.all_to_all(total, 'seq', 0, 0)]
  transfers between devices with their start and end apart: 3 -> 28, of which waited for: 3 -> 12; matrix products, arithmetic and copies ran while one was open for 5% -> 0% of each run, Pallas kernels for 0% -> 22%
where the time goes in v1:
time: 176 us; the launch traced here: 174 us
  Pallas kernels  69.6 us (40%)
  starting transfers between devices  45.9 us (26%)
  waiting for transfers between devices  43.2 us (25%)
  local copies, waits for them, and re-layouts  12.2 us (7%)
    pallas_call x8, Pallas kernels, half_grads(): pl.pallas_call(functools.partial(half_body, inner, block, len(pieces), ac...  44.5 us
    ppermute x15, waiting for transfers between devices, z_shift(): return lax.ppermute(array, 'tok', pairs)  34.5 us
    ppermute x15, starting transfers between devices, z_shift(): return lax.ppermute(array, 'tok', pairs)  18.5 us
    ppermute x11, starting transfers between devices, other_core(): return lax.ppermute(array, 'tok', [(t, t ^ 1) for t in range(parts)])  17.1 us
    pallas_call x2, Pallas kernels, output_of(): pl.pallas_call(functools.partial(output_body, block, len(pieces)), grid=(...  9.48 us
    pallas_call x3, Pallas kernels, combine(): pl.pallas_call(combine_body, grid=(1,), in_specs=[whole(own), whole(other...  7.8 us
    all_to_all x1, waiting for transfers between devices, per_device(): total = lax.all_to_all(total, 'seq', 0, 0)  7.61 us
    all_to_all x1, starting transfers between devices, per_device(): total = lax.all_to_all(total, 'seq', 0, 0)  6.75 us
  transfers between devices with their start and end apart: 28, of which 12 were waited for; matrix products, arithmetic and copies ran while one was open for 0% of the time, Pallas kernels for 22%

profile of v1, /device:TPU:1, one launch (start us, length us, event | category | flops | bytes accessed | tf_op | source)
XLA Modules:
  0.0 173.9 jit_solution(17955051089379846344)
XLA Ops:
  0.6 2.9 %prep.1.refs_3_ = bf16[2,4,3,64,512]{4,3,2,1,0:T(8,128)(2,1)} custom-call(s32[1]{0:T(128)} %bitcast.where_ref, bf16[512,512]{1,0:T(8,128)(2,1)} %gate_ref.1, bf16[512,512]{1,0:T(8,128)(2,1)} %up_ref.1, bf16[512,512]{1,0:T(8,128)(2,1)} %down_ref.1), custom_call_target="tpu_custom_call" | custom-call | tf_op jit(solution)/shard_map/prep/pallas_call | solution.py:54
  3.5 2.7 %slice_bitcast_fusion = (bf16[4,3,64,512]{3,2,1,0:T(8,128)(2,1)}, bf16[4,3,64,512]{3,2,1,0:T(8,128)(2,1)}) fusion(bf16[2,4,3,64,512]{4,3,2,1,0:T(8,128)(2,1)} %prep.1.refs_3_), kind=kLoop, calls=%fused_computation | loop fusion | bytes 3145728 | tf_op jit(solution)/shard_map/squeeze | solution.py:319
  6.8 5.2 %inner0.3 = bf16[3,256,512]{2,1,0:T(8,128)(2,1)} custom-call(s32[1]{0:T(128)} %bitcast.where_ref, s32[1,2]{1,0:T(1,128)} %count_ref.19, f32[1]{0:T(128)S(6)} %copy.20.scale_ref, f32[1,2,1024]{2,1,0:T(2,128)} %rate_ref.15, bf16[1,2,1024,512]{3,2,1,0:T(8,128)(2,1)} %x_ref.13, bf16[1,2,1024,512]{3,2,1,0:T(8,128)(2,1)} %e_ref.11, ...), custom_call_target="tpu_custom_call" | custom-call | flops 1610612736 | bytes 2097152 | tf_op jit(solution)/shard_map/inner0/pallas_call | solution.py:149
  13.5 5.5 %inner0.2.own_ref = f32[3,256,512]{2,1,0:T(8,128)} custom-call(s32[1]{0:T(128)} %bitcast.where_ref, s32[1,2]{1,0:T(1,128)} %count_ref.19, f32[1]{0:T(128)S(6)} %copy.20.scale_ref, f32[1,2,1024]{2,1,0:T(2,128)} %rate_ref.15, bf16[1,2,1024,512]{3,2,1,0:T(8,128)(2,1)} %x_ref.13, bf16[1,2,1024,512]{3,2,1,0:T(8,128)(2,1)} %e_ref.11, ...), custom_call_target="tpu_custom_call" | custom-call | flops 1610612736 | bytes 2097152 | tf_op jit(solution)/shard_map/inner0/pallas_call | solution.py:149
  19.9 2.6 %combine.3 = (f32[3,64,512]{2,1,0:T(8,128)}, bf16[3,64,512]{2,1,0:T(8,128)(2,1)}, bf16[3,64,512]{2,1,0:T(8,128)(2,1)}, bf16[3,64,512]{2,1,0:T(8,128)(2,1)}) custom-call(f32[3,256,512]{2,1,0:T(8,128)} %inner0.2.own_ref, bf16[3,256,512]{2,1,0:T(8,128)(2,1)} %copy-done.4), custom_call_target="tpu_custom_call" | custom-call | tf_op jit(solution)/shard_map/combine/pallas_call | solution.py:224
  24.2 3.3 %collective-permute-start.2 = (bf16[3,64,512]{2,1,0:T(8,128)(2,1)}, bf16[3,64,512]{2,1,0:T(8,128)(2,1)S(1)}, u32[]{:S(2)}, u32[]{:S(2)}) collective-permute-start(bf16[3,64,512]{2,1,0:T(8,128)(2,1)} %get-tuple-element.26), channel_id=1, source_target_pairs={{0,64},{16,80},{32,96},{48,112},{64,0},{80,16},{96,32},{112,48},{1... | collective-permute-start | bytes 589832 | tf_op jit(solution)/shard_map/ppermute | solution.py:305
  28.3 3.6 %collective-permute-done.1.refs_0_ = bf16[3,64,512]{2,1,0:T(8,128)(2,1)S(1)} collective-permute-done((bf16[3,64,512]{2,1,0:T(8,128)(2,1)}, bf16[3,64,512]{2,1,0:T(8,128)(2,1)S(1)}, u32[]{:S(2)}, u32[]{:S(2)}) %collective-permute-start.1) | collective-permute-done | bytes 196640 | tf_op jit(solution)/shard_map/ppermute | solution.py:305
  31.8 5.1 %collective-permute-done.2.refs_1_ = bf16[3,64,512]{2,1,0:T(8,128)(2,1)S(1)} collective-permute-done((bf16[3,64,512]{2,1,0:T(8,128)(2,1)}, bf16[3,64,512]{2,1,0:T(8,128)(2,1)S(1)}, u32[]{:S(2)}, u32[]{:S(2)}) %collective-permute-start.2) | collective-permute-done | bytes 196640 | tf_op jit(solution)/shard_map/ppermute | solution.py:305
  37.7 2.4 %update.2 = (bf16[1,3,64,512]{3,2,1,0:T(8,128)(2,1)}, f32[64,128]{1,0:T(8,128)}, f32[3,64,512]{2,1,0:T(8,128)}, f32[3,64,512]{2,1,0:T(8,128)}, f32[3,64,128]{2,1,0:T(8,128)}) custom-call(f32[1]{0:T(128)S(6)} %copy.20.scale_ref, f32[3,64,512]{2,1,0:T(8,128)} %get-tuple-element.24.own_ref, bf16[3,64,512]{2,1,0:T(8,128)(2,1)} %copy-done.20, ...), custom_call_target="tpu_custom_call" | custom-call | tf_op jit(solution)/shard_map/update/pallas_call | solution.py:284
  49.2 3.3 %collective-permute-start.8 = (bf16[1,3,64,512]{3,2,1,0:T(8,128)(2,1)S(1)}, bf16[1,3,64,512]{3,2,1,0:T(8,128)(2,1)S(1)}, u32[]{:S(2)}, u32[]{:S(2)}) collective-permute-start(bf16[1,3,64,512]{3,2,1,0:T(8,128)(2,1)S(1)} %collective-permute-done.4.refs_1_), channel_id=1, source_target_pairs={{0,16},{16,0},{32,48},{48,32},{64,80},{80,64},{96,112},{112,96},{1... | collective-permute-start | bytes 589832 | tf_op jit(solution)/shard_map/ppermute | solution.py:308
  55.4 5.2 %inner1.3 = bf16[3,256,512]{2,1,0:T(8,128)(2,1)} custom-call(s32[1]{0:T(128)} %bitcast.where_ref, s32[1,2]{1,0:T(1,128)} %count_ref.19, f32[1]{0:T(128)S(6)} %copy.20.scale_ref, f32[1,2,1024]{2,1,0:T(2,128)} %rate_ref.15, bf16[1,2,1024,512]{3,2,1,0:T(8,128)(2,1)} %x_ref.13, bf16[1,2,1024,512]{3,2,1,0:T(8,128)(2,1)} %e_ref.11, ...), custom_call_target="tpu_custom_call" | custom-call | flops 1610612736 | bytes 2097152 | tf_op jit(solution)/shard_map/inner1/pallas_call | solution.py:149
  61.1 5.5 %inner1.2.own_ref = f32[3,256,512]{2,1,0:T(8,128)} custom-call(s32[1]{0:T(128)} %bitcast.where_ref, s32[1,2]{1,0:T(1,128)} %count_ref.19, f32[1]{0:T(128)S(6)} %copy.20.scale_ref, f32[1,2,1024]{2,1,0:T(2,128)} %rate_ref.15, bf16[1,2,1024,512]{3,2,1,0:T(8,128)(2,1)} %x_ref.13, bf16[1,2,1024,512]{3,2,1,0:T(8,128)(2,1)} %e_ref.11, ...), custom_call_target="tpu_custom_call" | custom-call | flops 1610612736 | bytes 2097152 | tf_op jit(solution)/shard_map/inner1/pallas_call | solution.py:149
  67.5 2.6 %combine.4 = (f32[3,64,512]{2,1,0:T(8,128)}, bf16[3,64,512]{2,1,0:T(8,128)(2,1)}, bf16[3,64,512]{2,1,0:T(8,128)(2,1)}, bf16[3,64,512]{2,1,0:T(8,128)(2,1)}) custom-call(f32[3,256,512]{2,1,0:T(8,128)} %inner1.2.own_ref, bf16[3,256,512]{2,1,0:T(8,128)(2,1)} %copy-done.5), custom_call_target="tpu_custom_call" | custom-call | tf_op jit(solution)/shard_map/combine/pallas_call | solution.py:224
  71.0 3.1 %collective-permute-start.13 = (bf16[3,64,512]{2,1,0:T(8,128)(2,1)}, bf16[3,64,512]{2,1,0:T(8,128)(2,1)S(1)}, u32[]{:S(2)}, u32[]{:S(2)}) collective-permute-start(bf16[3,64,512]{2,1,0:T(8,128)(2,1)} %get-tuple-element.31), channel_id=1, source_target_pairs={{0,64},{16,80},{32,96},{48,112},{64,0},{80,16},{96,32},{112,48},{1... | collective-permute-start | bytes 589832 | tf_op jit(solution)/shard_map/ppermute | solution.py:305
  74.1 3.9 %collective-permute-done.12.refs_0_ = bf16[3,64,512]{2,1,0:T(8,128)(2,1)S(1)} collective-permute-done((bf16[3,64,512]{2,1,0:T(8,128)(2,1)}, bf16[3,64,512]{2,1,0:T(8,128)(2,1)S(1)}, u32[]{:S(2)}, u32[]{:S(2)}) %collective-permute-start.12) | collective-permute-done | bytes 196640 | tf_op jit(solution)/shard_map/ppermute | solution.py:305
  78.0 5.3 %collective-permute-done.13.refs_1_ = bf16[3,64,512]{2,1,0:T(8,128)(2,1)S(1)} collective-permute-done((bf16[3,64,512]{2,1,0:T(8,128)(2,1)}, bf16[3,64,512]{2,1,0:T(8,128)(2,1)S(1)}, u32[]{:S(2)}, u32[]{:S(2)}) %collective-permute-start.13) | collective-permute-done | bytes 196640 | tf_op jit(solution)/shard_map/ppermute | solution.py:305
  84.1 2.5 %update.3 = (bf16[1,3,64,512]{3,2,1,0:T(8,128)(2,1)}, f32[64,128]{1,0:T(8,128)}) custom-call(f32[1]{0:T(128)S(6)} %copy.20.scale_ref, f32[3,64,512]{2,1,0:T(8,128)} %get-tuple-element.29.own_ref, bf16[3,64,512]{2,1,0:T(8,128)(2,1)} %copy-done.17, bf16[3,64,512]{2,1,0:T(8,128)(2,1)} %copy-done.18, bf16[3,64,512]{2,1,0:T(8,128)(2,1)} %copy-done.19, ...), custom_call_target="tpu_custom_call" | custom-call | tf_op jit(solution)/shard_map/update/pallas_call | solution.py:284
  86.6 2.2 %collective-permute-start.15 = (bf16[1,3,64,512]{3,2,1,0:T(8,128)(2,1)}, bf16[1,3,64,512]{3,2,1,0:T(8,128)(2,1)S(1)}, u32[]{:S(2)}, u32[]{:S(2)}) collective-permute-start(bf16[1,3,64,512]{3,2,1,0:T(8,128)(2,1)} %get-tuple-element.36.refs_0_), channel_id=1, source_target_pairs={{0,96},{16,112},{32,0},{48,16},{64,32},{80,48},{96,64},{112,80},{1... | collective-permute-start | bytes 589832 | tf_op jit(solution)/shard_map/ppermute | solution.py:305
  90.5 3.5 %collective-permute-done.15.refs_1_ = bf16[1,3,64,512]{3,2,1,0:T(8,128)(2,1)S(1)} collective-permute-done((bf16[1,3,64,512]{3,2,1,0:T(8,128)(2,1)}, bf16[1,3,64,512]{3,2,1,0:T(8,128)(2,1)S(1)}, u32[]{:S(2)}, u32[]{:S(2)}) %collective-permute-start.15) | collective-permute-done | bytes 196640 | tf_op jit(solution)/shard_map/ppermute | solution.py:305
  94.0 4.5 %collective-permute-start.19 = (bf16[1,3,64,512]{3,2,1,0:T(8,128)(2,1)S(1)}, bf16[1,3,64,512]{3,2,1,0:T(8,128)(2,1)S(1)}, u32[]{:S(2)}, u32[]{:S(2)}) collective-permute-start(bf16[1,3,64,512]{3,2,1,0:T(8,128)(2,1)S(1)} %collective-permute-done.15.refs_1_), channel_id=1, source_target_pairs={{0,16},{16,0},{32,48},{48,32},{64,80},{80,64},{96,112},{112,96},{1... | collective-permute-start | bytes 589832 | tf_op jit(solution)/shard_map/ppermute | solution.py:308
  101.8 5.5 %outer0.3.refs_4_ = f32[3,256,512]{2,1,0:T(8,128)} custom-call(s32[1]{0:T(128)} %bitcast.where_ref, s32[1,2]{1,0:T(1,128)} %count_ref.19, f32[1]{0:T(128)S(6)} %copy.20.scale_ref, f32[1,2,1024]{2,1,0:T(2,128)} %rate_ref.15, bf16[1,2,1024,512]{3,2,1,0:T(8,128)(2,1)} %x_ref.19, bf16[1,2,1024,512]{3,2,1,0:T(8,128)(2,1)} %e_ref.15, ...), custom_call_target="tpu_custom_call" | custom-call | flops 1610612736 | bytes 2097152 | tf_op jit(solution)/shard_map/outer0/pallas_call | solution.py:149
  108.9 5.9 %outer1.3 = bf16[3,256,512]{2,1,0:T(8,128)(2,1)} custom-call(s32[1]{0:T(128)} %bitcast.where_ref, s32[1,2]{1,0:T(1,128)} %count_ref.19, f32[1]{0:T(128)S(6)} %copy.20.scale_ref, f32[1,2,1024]{2,1,0:T(2,128)} %rate_ref.15, bf16[1,2,1024,512]{3,2,1,0:T(8,128)(2,1)} %x_ref.19, bf16[1,2,1024,512]{3,2,1,0:T(8,128)(2,1)} %e_ref.15, ...), custom_call_target="tpu_custom_call" | custom-call | flops 1610612736 | bytes 2097152 | tf_op jit(solution)/shard_map/outer1/pallas_call | solution.py:149
  114.9 5.5 %outer0.2.refs_4_ = f32[3,256,512]{2,1,0:T(8,128)} custom-call(s32[1]{0:T(128)} %bitcast.where_ref, s32[1,2]{1,0:T(1,128)} %count_ref.19, f32[1]{0:T(128)S(6)} %copy.20.scale_ref, f32[1,2,1024]{2,1,0:T(2,128)} %rate_ref.15, bf16[1,2,1024,512]{3,2,1,0:T(8,128)(2,1)} %x_ref.19, bf16[1,2,1024,512]{3,2,1,0:T(8,128)(2,1)} %e_ref.15, ...), custom_call_target="tpu_custom_call" | custom-call | flops 1610612736 | bytes 2097152 | tf_op jit(solution)/shard_map/outer0/pallas_call | solution.py:149
  120.4 6.2 %outer1.2.own_ref = f32[3,256,512]{2,1,0:T(8,128)} custom-call(s32[1]{0:T(128)} %bitcast.where_ref, s32[1,2]{1,0:T(1,128)} %count_ref.19, f32[1]{0:T(128)S(6)} %copy.20.scale_ref, f32[1,2,1024]{2,1,0:T(2,128)} %rate_ref.15, bf16[1,2,1024,512]{3,2,1,0:T(8,128)(2,1)} %x_ref.19, bf16[1,2,1024,512]{3,2,1,0:T(8,128)(2,1)} %e_ref.15, ...), custom_call_target="tpu_custom_call" | custom-call | flops 1610612736 | bytes 2097152 | tf_op jit(solution)/shard_map/outer1/pallas_call | solution.py:149
  127.5 2.6 %combine.5 = (f32[3,64,512]{2,1,0:T(8,128)}, bf16[3,64,512]{2,1,0:T(8,128)(2,1)}, bf16[3,64,512]{2,1,0:T(8,128)(2,1)}, bf16[3,64,512]{2,1,0:T(8,128)(2,1)}) custom-call(f32[3,256,512]{2,1,0:T(8,128)} %outer1.2.own_ref, bf16[3,256,512]{2,1,0:T(8,128)(2,1)} %copy-done.3), custom_call_target="tpu_custom_call" | custom-call | tf_op jit(solution)/shard_map/combine/pallas_call | solution.py:224
  133.0 5.5 %collective-permute-done.23 = bf16[3,64,512]{2,1,0:T(8,128)(2,1)S(1)} collective-permute-done((bf16[3,64,512]{2,1,0:T(8,128)(2,1)}, bf16[3,64,512]{2,1,0:T(8,128)(2,1)S(1)}, u32[]{:S(2)}, u32[]{:S(2)}) %collective-permute-start.23) | collective-permute-done | bytes 196640 | tf_op jit(solution)/shard_map/ppermute | solution.py:305
  138.4 2.5 %collective-permute-done.24 = bf16[3,64,512]{2,1,0:T(8,128)(2,1)S(1)} collective-permute-done((bf16[3,64,512]{2,1,0:T(8,128)(2,1)}, bf16[3,64,512]{2,1,0:T(8,128)(2,1)S(1)}, u32[]{:S(2)}, u32[]{:S(2)}) %collective-permute-start.24) | collective-permute-done | bytes 196640 | tf_op jit(solution)/shard_map/ppermute | solution.py:305
  144.0 6.8 %all-to-all-start = ((bf16[16,12,512]{2,1,0:T(8,128)(2,1)}), bf16[16,12,512]{2,1,0:T(8,128)(2,1)S(1)}, u32[]{:S(2)}, u32[]{:S(2)}) async-start(bf16[16,12,512]{2,1,0:T(8,128)(2,1)} %reshape.24), calls=%async_computation | async-start | bytes 524288 | tf_op jit(solution)/shard_map/all_to_all | solution.py:348
  150.8 7.6 %all-to-all-done = bf16[16,12,512]{2,1,0:T(8,128)(2,1)S(1)} async-done(((bf16[16,12,512]{2,1,0:T(8,128)(2,1)}), bf16[16,12,512]{2,1,0:T(8,128)(2,1)S(1)}, u32[]{:S(2)}, u32[]{:S(2)}) %all-to-all-start) | async-done | bytes 196640 | tf_op jit(solution)/shard_map/all_to_all | solution.py:348
  159.3 3.5 %all-to-all-start.1 = ((bf16[16,13,512]{2,1,0:T(8,128)(2,1)}), bf16[16,13,512]{2,1,0:T(8,128)(2,1)S(1)}, u32[]{:S(2)}, u32[]{:S(2)}) async-start(bf16[16,13,512]{2,1,0:T(8,128)(2,1)} %broadcast_in_dim.14), calls=%async_computation.1 | async-start | bytes 524288 | tf_op jit(solution)/shard_map/all_to_all | solution.py:357
  162.8 4.7 %output0.1.refs_8_ = bf16[1,2,1024,512]{3,2,1,0:T(8,128)(2,1)} custom-call(s32[1]{0:T(128)} %bitcast.where_ref, s32[1,2]{1,0:T(1,128)} %count_ref.19, bf16[1,2,1024,512]{3,2,1,0:T(8,128)(2,1)} %x_ref.19, bf16[1,3,64,512]{3,2,1,0:T(8,128)(2,1)} %get-tuple-element.28.refs_0_, bf16[1,3,64,512]{3,2,1,0:T(8,128)(2,1)} %copy-done.1, ...), custom_call_target="tpu_custom_call" | custom-call | flops 1610612736 | bytes 2097152 | tf_op jit(solution)/shard_map/output0/pallas_call | solution.py:198
  167.5 4.7 %output1.1 = bf16[1,2,1024,512]{3,2,1,0:T(8,128)(2,1)} custom-call(s32[1]{0:T(128)} %bitcast.where_ref, s32[1,2]{1,0:T(1,128)} %count_ref.19, bf16[1,2,1024,512]{3,2,1,0:T(8,128)(2,1)} %x_ref.19, bf16[1,3,64,512]{3,2,1,0:T(8,128)(2,1)} %get-tuple-element.36.refs_0_, bf16[1,3,64,512]{3,2,1,0:T(8,128)(2,1)} %copy-done.6, ...), custom_call_target="tpu_custom_call", output_to_operand_aliasing={{}: (11, {})} | custom-call | flops 1610612736 | bytes 2097152 | tf_op jit(solution)/shard_map/output1/pallas_call | solution.py:198
  (110 shorter events, 36.3 us)
Async XLA Ops:
  12.1 6.9 %collective-permute-start = (bf16[3,256,512]{2,1,0:T(8,128)(2,1)}, bf16[3,256,512]{2,1,0:T(8,128)(2,1)S(1)}, u32[]{:S(2)}, u32[]{:S(2)}) collective-permute-start(bf16[3,256,512]{2,1,0:T(8,128)(2,1)} %inner0.3), channel_id=1, source_target_pairs={{0,16},{16,0},{32,48},{48,32},{64,80},{80,64},{96,112},{112,96},{1... | collective-permute-start | bytes 2359304 | tf_op jit(solution)/shard_map/ppermute | solution.py:308
  22.5 9.3 %collective-permute-start.1 = (bf16[3,64,512]{2,1,0:T(8,128)(2,1)}, bf16[3,64,512]{2,1,0:T(8,128)(2,1)S(1)}, u32[]{:S(2)}, u32[]{:S(2)}) collective-permute-start(bf16[3,64,512]{2,1,0:T(8,128)(2,1)} %get-tuple-element.25), channel_id=1, source_target_pairs={{0,32},{16,48},{32,64},{48,80},{64,96},{80,112},{96,0},{112,16},{1... | collective-permute-start | bytes 589832 | tf_op jit(solution)/shard_map/ppermute | solution.py:305
  24.2 12.7 %collective-permute-start.2 = (bf16[3,64,512]{2,1,0:T(8,128)(2,1)}, bf16[3,64,512]{2,1,0:T(8,128)(2,1)S(1)}, u32[]{:S(2)}, u32[]{:S(2)}) collective-permute-start(bf16[3,64,512]{2,1,0:T(8,128)(2,1)} %get-tuple-element.26), channel_id=1, source_target_pairs={{0,64},{16,80},{32,96},{48,112},{64,0},{80,16},{96,32},{112,48},{1... | collective-permute-start | bytes 589832 | tf_op jit(solution)/shard_map/ppermute | solution.py:305
  27.5 9.4 %collective-permute-start.3 = (bf16[3,64,512]{2,1,0:T(8,128)(2,1)}, bf16[3,64,512]{2,1,0:T(8,128)(2,1)S(1)}, u32[]{:S(2)}, u32[]{:S(2)}) collective-permute-start(bf16[3,64,512]{2,1,0:T(8,128)(2,1)} %get-tuple-element.27), channel_id=1, source_target_pairs={{0,96},{16,112},{32,0},{48,16},{64,32},{80,48},{96,64},{112,80},{1... | collective-permute-start | bytes 589832 | tf_op jit(solution)/shard_map/ppermute | solution.py:305
  40.1 7.0 %collective-permute-start.6 = (bf16[1,3,64,512]{3,2,1,0:T(8,128)(2,1)}, bf16[1,3,64,512]{3,2,1,0:T(8,128)(2,1)S(1)}, u32[]{:S(2)}, u32[]{:S(2)}) collective-permute-start(bf16[1,3,64,512]{3,2,1,0:T(8,128)(2,1)} %get-tuple-element.28.refs_0_), channel_id=1, source_target_pairs={{0,32},{16,48},{32,64},{48,80},{64,96},{80,112},{96,0},{112,16},{1... | collective-permute-start | bytes 589832 | tf_op jit(solution)/shard_map/ppermute | solution.py:305
  40.9 8.4 %collective-permute-start.4 = (bf16[1,3,64,512]{3,2,1,0:T(8,128)(2,1)}, bf16[1,3,64,512]{3,2,1,0:T(8,128)(2,1)S(1)}, u32[]{:S(2)}, u32[]{:S(2)}) collective-permute-start(bf16[1,3,64,512]{3,2,1,0:T(8,128)(2,1)} %get-tuple-element.28.refs_0_), channel_id=1, source_target_pairs={{0,96},{16,112},{32,0},{48,16},{64,32},{80,48},{96,64},{112,80},{1... | collective-permute-start | bytes 589832 | tf_op jit(solution)/shard_map/ppermute | solution.py:305
  42.8 9.7 %collective-permute-start.5 = (bf16[1,3,64,512]{3,2,1,0:T(8,128)(2,1)}, bf16[1,3,64,512]{3,2,1,0:T(8,128)(2,1)S(1)}, u32[]{:S(2)}, u32[]{:S(2)}) collective-permute-start(bf16[1,3,64,512]{3,2,1,0:T(8,128)(2,1)} %get-tuple-element.28.refs_0_), channel_id=1, source_target_pairs={{0,64},{16,80},{32,96},{48,112},{64,0},{80,16},{96,32},{112,48},{1... | collective-permute-start | bytes 589832 | tf_op jit(solution)/shard_map/ppermute | solution.py:305
  43.4 10.3 %collective-permute-start.7 = (bf16[1,3,64,512]{3,2,1,0:T(8,128)(2,1)}, bf16[1,3,64,512]{3,2,1,0:T(8,128)(2,1)S(1)}, u32[]{:S(2)}, u32[]{:S(2)}) collective-permute-start(bf16[1,3,64,512]{3,2,1,0:T(8,128)(2,1)} %get-tuple-element.28.refs_0_), channel_id=1, source_target_pairs={{0,16},{16,0},{32,48},{48,32},{64,80},{80,64},{96,112},{112,96},{1... | collective-permute-start | bytes 589832 | tf_op jit(solution)/shard_map/ppermute | solution.py:308
  47.1 13.5 %copy-start = (bf16[1,3,64,512]{3,2,1,0:T(8,128)(2,1)}, bf16[1,3,64,512]{3,2,1,0:T(8,128)(2,1)S(1)}, u32[]{:S(2)}) copy-start(bf16[1,3,64,512]{3,2,1,0:T(8,128)(2,1)S(1)} %collective-permute-done.6.refs_3_) | copy-start | bytes 589828
  47.1 6.6 %collective-permute-start.10 = (bf16[1,3,64,512]{3,2,1,0:T(8,128)(2,1)S(1)}, bf16[1,3,64,512]{3,2,1,0:T(8,128)(2,1)S(1)}, u32[]{:S(2)}, u32[]{:S(2)}) collective-permute-start(bf16[1,3,64,512]{3,2,1,0:T(8,128)(2,1)S(1)} %collective-permute-done.6.refs_3_), channel_id=1, source_target_pairs={{0,16},{16,0},{32,48},{48,32},{64,80},{80,64},{96,112},{112,96},{1... | collective-permute-start | bytes 589832 | tf_op jit(solution)/shard_map/ppermute | solution.py:308
  49.2 11.5 %copy-start.1 = (bf16[1,3,64,512]{3,2,1,0:T(8,128)(2,1)}, bf16[1,3,64,512]{3,2,1,0:T(8,128)(2,1)S(1)}, u32[]{:S(2)}) copy-start(bf16[1,3,64,512]{3,2,1,0:T(8,128)(2,1)S(1)} %collective-permute-done.4.refs_1_) | copy-start | bytes 589828
  49.2 4.5 %collective-permute-start.8 = (bf16[1,3,64,512]{3,2,1,0:T(8,128)(2,1)S(1)}, bf16[1,3,64,512]{3,2,1,0:T(8,128)(2,1)S(1)}, u32[]{:S(2)}, u32[]{:S(2)}) collective-permute-start(bf16[1,3,64,512]{3,2,1,0:T(8,128)(2,1)S(1)} %collective-permute-done.4.refs_1_), channel_id=1, source_target_pairs={{0,16},{16,0},{32,48},{48,32},{64,80},{80,64},{96,112},{112,96},{1... | collective-permute-start | bytes 589832 | tf_op jit(solution)/shard_map/ppermute | solution.py:308
  52.5 2.3 %collective-permute-start.9 = (bf16[1,3,64,512]{3,2,1,0:T(8,128)(2,1)S(1)}, bf16[1,3,64,512]{3,2,1,0:T(8,128)(2,1)S(1)}, u32[]{:S(2)}, u32[]{:S(2)}) collective-permute-start(bf16[1,3,64,512]{3,2,1,0:T(8,128)(2,1)S(1)} %collective-permute-done.5.refs_2_), channel_id=1, source_target_pairs={{0,16},{16,0},{32,48},{48,32},{64,80},{80,64},{96,112},{112,96},{1... | collective-permute-start | bytes 589832 | tf_op jit(solution)/shard_map/ppermute | solution.py:308
  60.7 6.0 %collective-permute-start.11 = (bf16[3,256,512]{2,1,0:T(8,128)(2,1)}, bf16[3,256,512]{2,1,0:T(8,128)(2,1)S(1)}, u32[]{:S(2)}, u32[]{:S(2)}) collective-permute-start(bf16[3,256,512]{2,1,0:T(8,128)(2,1)} %inner1.3), channel_id=1, source_target_pairs={{0,16},{16,0},{32,48},{48,32},{64,80},{80,64},{96,112},{112,96},{1... | collective-permute-start | bytes 2359304 | tf_op jit(solution)/shard_map/ppermute | solution.py:308
  70.2 7.9 %collective-permute-start.12 = (bf16[3,64,512]{2,1,0:T(8,128)(2,1)}, bf16[3,64,512]{2,1,0:T(8,128)(2,1)S(1)}, u32[]{:S(2)}, u32[]{:S(2)}) collective-permute-start(bf16[3,64,512]{2,1,0:T(8,128)(2,1)} %get-tuple-element.30), channel_id=1, source_target_pairs={{0,32},{16,48},{32,64},{48,80},{64,96},{80,112},{96,0},{112,16},{1... | collective-permute-start | bytes 589832 | tf_op jit(solution)/shard_map/ppermute | solution.py:305
  71.0 12.3 %collective-permute-start.13 = (bf16[3,64,512]{2,1,0:T(8,128)(2,1)}, bf16[3,64,512]{2,1,0:T(8,128)(2,1)S(1)}, u32[]{:S(2)}, u32[]{:S(2)}) collective-permute-start(bf16[3,64,512]{2,1,0:T(8,128)(2,1)} %get-tuple-element.31), channel_id=1, source_target_pairs={{0,64},{16,80},{32,96},{48,112},{64,0},{80,16},{96,32},{112,48},{1... | collective-permute-start | bytes 589832 | tf_op jit(solution)/shard_map/ppermute | solution.py:305
  74.1 9.3 %collective-permute-start.14 = (bf16[3,64,512]{2,1,0:T(8,128)(2,1)}, bf16[3,64,512]{2,1,0:T(8,128)(2,1)S(1)}, u32[]{:S(2)}, u32[]{:S(2)}) collective-permute-start(bf16[3,64,512]{2,1,0:T(8,128)(2,1)} %get-tuple-element.32), channel_id=1, source_target_pairs={{0,96},{16,112},{32,0},{48,16},{64,32},{80,48},{96,64},{112,80},{1... | collective-permute-start | bytes 589832 | tf_op jit(solution)/shard_map/ppermute | solution.py:305
  86.6 7.4 %collective-permute-start.15 = (bf16[1,3,64,512]{3,2,1,0:T(8,128)(2,1)}, bf16[1,3,64,512]{3,2,1,0:T(8,128)(2,1)S(1)}, u32[]{:S(2)}, u32[]{:S(2)}) collective-permute-start(bf16[1,3,64,512]{3,2,1,0:T(8,128)(2,1)} %get-tuple-element.36.refs_0_), channel_id=1, source_target_pairs={{0,96},{16,112},{32,0},{48,16},{64,32},{80,48},{96,64},{112,80},{1... | collective-permute-start | bytes 589832 | tf_op jit(solution)/shard_map/ppermute | solution.py:305
  88.9 9.7 %collective-permute-start.16 = (bf16[1,3,64,512]{3,2,1,0:T(8,128)(2,1)}, bf16[1,3,64,512]{3,2,1,0:T(8,128)(2,1)S(1)}, u32[]{:S(2)}, u32[]{:S(2)}) collective-permute-start(bf16[1,3,64,512]{3,2,1,0:T(8,128)(2,1)} %get-tuple-element.36.refs_0_), channel_id=1, source_target_pairs={{0,64},{16,80},{32,96},{48,112},{64,0},{80,16},{96,32},{112,48},{1... | collective-permute-start | bytes 589832 | tf_op jit(solution)/shard_map/ppermute | solution.py:305
  88.9 12.2 %collective-permute-start.17 = (bf16[1,3,64,512]{3,2,1,0:T(8,128)(2,1)}, bf16[1,3,64,512]{3,2,1,0:T(8,128)(2,1)S(1)}, u32[]{:S(2)}, u32[]{:S(2)}) collective-permute-start(bf16[1,3,64,512]{3,2,1,0:T(8,128)(2,1)} %get-tuple-element.36.refs_0_), channel_id=1, source_target_pairs={{0,32},{16,48},{32,64},{48,80},{64,96},{80,112},{96,0},{112,16},{1... | collective-permute-start | bytes 589832 | tf_op jit(solution)/shard_map/ppermute | solution.py:305
  89.5 17.9 %collective-permute-start.18 = (bf16[1,3,64,512]{3,2,1,0:T(8,128)(2,1)}, bf16[1,3,64,512]{3,2,1,0:T(8,128)(2,1)S(1)}, u32[]{:S(2)}, u32[]{:S(2)}) collective-permute-start(bf16[1,3,64,512]{3,2,1,0:T(8,128)(2,1)} %get-tuple-element.36.refs_0_), channel_id=1, source_target_pairs={{0,16},{16,0},{32,48},{48,32},{64,80},{80,64},{96,112},{112,96},{1... | collective-permute-start | bytes 589832 | tf_op jit(solution)/shard_map/ppermute | solution.py:308
  94.0 13.3 %copy-start.6 = (bf16[1,3,64,512]{3,2,1,0:T(8,128)(2,1)}, bf16[1,3,64,512]{3,2,1,0:T(8,128)(2,1)S(1)}, u32[]{:S(2)}) copy-start(bf16[1,3,64,512]{3,2,1,0:T(8,128)(2,1)S(1)} %collective-permute-done.15.refs_1_) | copy-start | bytes 589828
  94.0 13.3 %collective-permute-start.19 = (bf16[1,3,64,512]{3,2,1,0:T(8,128)(2,1)S(1)}, bf16[1,3,64,512]{3,2,1,0:T(8,128)(2,1)S(1)}, u32[]{:S(2)}, u32[]{:S(2)}) collective-permute-start(bf16[1,3,64,512]{3,2,1,0:T(8,128)(2,1)S(1)} %collective-permute-done.15.refs_1_), channel_id=1, source_target_pairs={{0,16},{16,0},{32,48},{48,32},{64,80},{80,64},{96,112},{112,96},{1... | collective-permute-start | bytes 589832 | tf_op jit(solution)/shard_map/ppermute | solution.py:308
  98.6 8.8 %copy-start.7 = (bf16[1,3,64,512]{3,2,1,0:T(8,128)(2,1)}, bf16[1,3,64,512]{3,2,1,0:T(8,128)(2,1)S(1)}, u32[]{:S(2)}) copy-start(bf16[1,3,64,512]{3,2,1,0:T(8,128)(2,1)S(1)} %collective-permute-done.16.refs_2_) | copy-start | bytes 589828
  98.6 8.8 %collective-permute-start.20 = (bf16[1,3,64,512]{3,2,1,0:T(8,128)(2,1)S(1)}, bf16[1,3,64,512]{3,2,1,0:T(8,128)(2,1)S(1)}, u32[]{:S(2)}, u32[]{:S(2)}) collective-permute-start(bf16[1,3,64,512]{3,2,1,0:T(8,128)(2,1)S(1)} %collective-permute-done.16.refs_2_), channel_id=1, source_target_pairs={{0,16},{16,0},{32,48},{48,32},{64,80},{80,64},{96,112},{112,96},{1... | collective-permute-start | bytes 589832 | tf_op jit(solution)/shard_map/ppermute | solution.py:308
  101.1 6.4 %collective-permute-start.21 = (bf16[1,3,64,512]{3,2,1,0:T(8,128)(2,1)S(1)}, bf16[1,3,64,512]{3,2,1,0:T(8,128)(2,1)S(1)}, u32[]{:S(2)}, u32[]{:S(2)}) collective-permute-start(bf16[1,3,64,512]{3,2,1,0:T(8,128)(2,1)S(1)} %collective-permute-done.17.refs_3_), channel_id=1, source_target_pairs={{0,16},{16,0},{32,48},{48,32},{64,80},{80,64},{96,112},{112,96},{1... | collective-permute-start | bytes 589832 | tf_op jit(solution)/shard_map/ppermute | solution.py:308
  114.7 11.9 %collective-permute-start.22 = (bf16[3,256,512]{2,1,0:T(8,128)(2,1)}, bf16[3,256,512]{2,1,0:T(8,128)(2,1)S(1)}, u32[]{:S(2)}, u32[]{:S(2)}) collective-permute-start(bf16[3,256,512]{2,1,0:T(8,128)(2,1)} %outer1.3), channel_id=1, source_target_pairs={{0,16},{16,0},{32,48},{48,32},{64,80},{80,64},{96,112},{112,96},{1... | collective-permute-start | bytes 2359304 | tf_op jit(solution)/shard_map/ppermute | solution.py:308
  130.1 8.3 %collective-permute-start.23 = (bf16[3,64,512]{2,1,0:T(8,128)(2,1)}, bf16[3,64,512]{2,1,0:T(8,128)(2,1)S(1)}, u32[]{:S(2)}, u32[]{:S(2)}) collective-permute-start(bf16[3,64,512]{2,1,0:T(8,128)(2,1)} %get-tuple-element.38), channel_id=1, source_target_pairs={{0,32},{16,48},{32,64},{48,80},{64,96},{80,112},{96,0},{112,16},{1... | collective-permute-start | bytes 589832 | tf_op jit(solution)/shard_map/ppermute | solution.py:305
  130.1 10.8 %collective-permute-start.24 = (bf16[3,64,512]{2,1,0:T(8,128)(2,1)}, bf16[3,64,512]{2,1,0:T(8,128)(2,1)S(1)}, u32[]{:S(2)}, u32[]{:S(2)}) collective-permute-start(bf16[3,64,512]{2,1,0:T(8,128)(2,1)} %get-tuple-element.39), channel_id=1, source_target_pairs={{0,64},{16,80},{32,96},{48,112},{64,0},{80,16},{96,32},{112,48},{1... | collective-permute-start | bytes 589832 | tf_op jit(solution)/shard_map/ppermute | solution.py:305
  131.9 10.3 %collective-permute-start.25 = (bf16[3,64,512]{2,1,0:T(8,128)(2,1)}, bf16[3,64,512]{2,1,0:T(8,128)(2,1)S(1)}, u32[]{:S(2)}, u32[]{:S(2)}) collective-permute-start(bf16[3,64,512]{2,1,0:T(8,128)(2,1)} %get-tuple-element.40), channel_id=1, source_target_pairs={{0,96},{16,112},{32,0},{48,16},{64,32},{80,48},{96,64},{112,80},{1... | collective-permute-start | bytes 589832 | tf_op jit(solution)/shard_map/ppermute | solution.py:305
  144.0 14.4 %all-to-all-start = ((bf16[16,12,512]{2,1,0:T(8,128)(2,1)}), bf16[16,12,512]{2,1,0:T(8,128)(2,1)S(1)}, u32[]{:S(2)}, u32[]{:S(2)}) async-start(bf16[16,12,512]{2,1,0:T(8,128)(2,1)} %reshape.24), calls=%async_computation | async-start | bytes 524288 | tf_op jit(solution)/shard_map/all_to_all | solution.py:348
  159.3 13.0 %all-to-all-start.1 = ((bf16[16,13,512]{2,1,0:T(8,128)(2,1)}), bf16[16,13,512]{2,1,0:T(8,128)(2,1)S(1)}, u32[]{:S(2)}, u32[]{:S(2)}) async-start(bf16[16,13,512]{2,1,0:T(8,128)(2,1)} %broadcast_in_dim.14), calls=%async_computation.1 | async-start | bytes 524288 | tf_op jit(solution)/shard_map/all_to_all | solution.py:357
  (21 other events, 50.9 us)

commit v2 on v0

v2 whole, which is shorter than its diff:
```python
import functools
import jax
import jax.numpy as jnp
from jax import lax
from jax.experimental import pallas as pl
from jax.experimental.pallas import tpu as pltpu
from jax.sharding import PartitionSpec as P


KEEP = 0.9
RATE = 3.0
TINY = 1e-06
BF = jnp.bfloat16
F32 = jnp.float32
NT = (((1,), (1,)), ((), ()))
TN = (((0,), (0,)), ((), ()))
MIB = 1024 * 1024
TILE = 512


def dot(a, b, dims=None):
    if dims is None:
        return jnp.dot(a, b, preferred_element_type=F32)
    return lax.dot_general(a, b, dims, preferred_element_type=F32)


VMEM = pl.BlockSpec(memory_space=pltpu.VMEM)
SMEM = pl.BlockSpec(memory_space=pltpu.SMEM)


def call(body, operands, n_smem, outs, scratch=(), limit=8, flops=0, n_exp=0):
    shapes = [jax.ShapeDtypeStruct(s, t) for s, t in outs]
    cost = None
    if flops:
        cost = pl.CostEstimate(flops=flops, transcendentals=n_exp, bytes_accessed=4 * MIB)
    return pl.pallas_call(
        body,
        in_specs=[SMEM] * n_smem + [VMEM] * (len(operands) - n_smem),
        out_specs=[VMEM] * len(shapes),
        out_shape=shapes,
        scratch_shapes=list(scratch),
        cost_estimate=cost,
        compiler_params=pltpu.CompilerParams(vmem_limit_bytes=limit * MIB),
    )(*operands)


def prep_body(where_ref, gate_ref, up_ref, down_ref, *refs):
    outs = refs[:2]
    gate_t, up_t = refs[2:]
    gate_t[...] = gate_ref[...].T
    up_t[...] = up_ref[...].T
    where = where_ref[0]
    z = where // 2
    core = where % 2
    chips, _, width, _ = outs[0].shape
    for half in range(2):
        for k in range(chips):
            owner = 2 * ((z + k) % chips) + (core + half) % 2
            rows = pl.ds(pl.multiple_of(owner * width, width), width)
            outs[half][k, 0] = gate_t[rows, :]
            outs[half][k, 1] = up_t[rows, :]
            outs[half][k, 2] = down_ref[rows, :]


def prep(where, w_gate, w_up, w_down, parts):
    dim, hid = w_gate.shape
    shape = (parts // 2, 3, hid // parts, dim)
    return call(
        prep_body,
        (where, w_gate, w_up, w_down),
        1,
        [(shape, BF)] * 2,
        scratch=[pltpu.VMEM((hid, dim), BF)] * 2,
    )


def gather_rows(pieces, gu, down):
    k = 0
    rows = down.shape[0]
    for ref in pieces:
        n, _, width, _ = ref.shape
        for i in range(n):
            gu[k * width : (k + 1) * width] = ref[i, 0]
            gu[rows + k * width : rows + (k + 1) * width] = ref[i, 1]
            down[k * width : (k + 1) * width] = ref[i, 2]
            k += 1


def mask_row(where, count, start, size, tokens):
    base = where * tokens + start
    return base + lax.broadcasted_iota(jnp.int32, (1, size), 1) < count


def grads_body(inner, block, n_pieces, skip, result, where_ref, count_ref, scale_ref, rate_ref, x_ref, e_ref, *refs):
    pieces = refs[:n_pieces]
    refs = refs[n_pieces:]
    has_acc = skip is not None
    if has_acc:
        start_ref = refs[0]
        refs = refs[1:]
    if result:
        out_ref, result_ref, gu, down, acc = refs
    else:
        out_ref, gu, down, acc = refs
    gather_rows(pieces, gu, down)
    rows = down.shape[0]
    tokens = x_ref.shape[2]
    count = count_ref[0, block]
    steps = tokens // TILE
    for i in range(steps):
        span = slice(i * TILE, (i + 1) * TILE)
        x = x_ref[0, block, span]
        e = e_ref[0, block, span]
        valid = mask_row(where_ref[0], count, i * TILE, TILE, tokens)
        if inner:
            factor = -(scale_ref[0] / count.astype(F32))
            row = jnp.where(valid, rate_ref[0, block : block + 1, span] * factor, 0.0)
        else:
            row = jnp.where(valid, 1.0, 0.0)
        ab = dot(gu[...], x, NT)
        a = ab[:rows]
        b = ab[rows:]
        r = dot(down[...], e, NT) * row
        s = 0.5 + 0.5 * jnp.tanh(0.5 * a)
        act = a * s
        hidden = (act * b * row).astype(BF)
        e_up = (r * act).astype(BF)
        e_gate = (r * b * (s + act * (1.0 - s))).astype(BF)
        for j, (left, right) in enumerate(((e_gate, x), (e_up, x), (hidden, e))):
            value = dot(left, right)
            if i > 0:
                value = value + acc[j]
            elif has_acc:
                value = value + start_ref[j, skip : skip + rows]
            if i == steps - 1:
                out_ref[j] = value.astype(out_ref.dtype)
            else:
                acc[j] = value
        if result:
            result_ref[span] = dot(hidden, down[...], TN).astype(BF)


def grads(inner, block, args, x, e, pieces, out_dtype, acc=None, skip=None, result=False):
    tokens, dim = x.shape[2:]
    n_rows = sum(p.shape[0] * p.shape[2] for p in pieces)
    shape = (3, n_rows, dim)
    operands = [*args, x, e, *pieces]
    if acc is not None:
        operands.append(acc)
    outs = [(shape, out_dtype)]
    if result:
        outs.append(((tokens, dim), BF))
    return call(
        functools.partial(grads_body, inner, block, len(pieces), skip, result),
        operands,
        3,
        outs,
        scratch=[pltpu.VMEM((2 * n_rows, dim), BF), pltpu.VMEM((n_rows, dim), BF), pltpu.VMEM(shape, F32)],
        limit=20,
        flops=12 * tokens * n_rows * dim,
        n_exp=tokens * n_rows,
    )


def output_body(block, n_pieces, where_ref, count_ref, x_ref, done_ref, *refs):
    out_ref, gu, down = refs[-3:]
    gather_rows(refs[:n_pieces], gu, down)
    rows = down.shape[0]
    tokens = x_ref.shape[2]
    for other in range(block):
        out_ref[0, other] = done_ref[...]
    for i in range(tokens // TILE):
        span = slice(i * TILE, (i + 1) * TILE)
        valid = mask_row(where_ref[0], count_ref[0, block], i * TILE, TILE, tokens)
        ab = dot(gu[...], x_ref[0, block, span], NT)
        a = ab[:rows]
        s = 0.5 + 0.5 * jnp.tanh(0.5 * a)
        hidden = jnp.where(valid, a * s * ab[rows:], 0.0).astype(BF)
        out_ref[0, block, span] = dot(hidden, down[...], TN).astype(BF)


def output_of(where, count, x, done, pieces):
    tokens, dim = x.shape[2:]
    n_rows = sum(p.shape[0] * p.shape[2] for p in pieces)
    return call(
        functools.partial(output_body, 1, len(pieces)),
        [where, count, x, done, *pieces],
        2,
        [(x.shape, BF)],
        scratch=[pltpu.VMEM((2 * n_rows, dim), BF), pltpu.VMEM((n_rows, dim), BF)],
        limit=16,
        flops=6 * tokens * n_rows * dim,
        n_exp=tokens * n_rows,
    )[0]


def combine_body(own_ref, other_ref, *outs):
    width = outs[0].shape[1]
    for k, out in enumerate(outs):
        rows = slice(k * width, (k + 1) * width)
        out[...] = (own_ref[:, rows, :].astype(F32) + other_ref[:, rows, :].astype(F32)).astype(out.dtype)


def combine(own, other, chips):
    shape = (3, own.shape[1] // chips, own.shape[2])
    outs = [(shape, F32 if k == 0 else BF) for k in range(chips)]
    return call(combine_body, (own, other), 0, outs)


def norm_of(w):
    return jnp.sqrt(jnp.sum(w * w, axis=1, keepdims=True) + TINY)


def update_body(first, n_recv, scale_ref, own_ref, *refs):
    recv = refs[:n_recv]
    refs = refs[n_recv:]
    if first:
        start_ref, piece_ref, level_ref, state_out, momentum_out, norm_out = refs
    else:
        state_ref, momentum_ref, norm_ref, piece_ref, level_ref = refs
    scale = scale_ref[0]
    for j in range(3):
        total = own_ref[j]
        for ref in recv:
            total = total + ref[j].astype(F32)
        if j == 0:
            level = jnp.max(jnp.abs(total), axis=1, keepdims=True)
            level = jnp.broadcast_to(level, (level.shape[0], 128)).T
            level_ref[...] = level[: level_ref.shape[0]]
        if first:
            state = start_ref[0, j].astype(F32)
            norm = norm_of(state)
            moved = total / scale
        else:
            state = state_ref[j]
            norm = norm_ref[j][:, :1]
            moved = KEEP * momentum_ref[j] + total / scale
        state = state - RATE * moved
        state = state * (norm / norm_of(state))
        piece_ref[0, j] = state.astype(BF)
        if first:
            state_out[j] = state
            momentum_out[j] = moved
            norm_out[j] = jnp.broadcast_to(norm, norm_out.shape[1:])


def update(scale, own, recv, start=None, carried=None):
    first = start is not None
    operands = [scale, own, *recv] + ([start] if first else list(carried))
    outs = [((1,) + own.shape, BF), ((8, own.shape[1]), F32)]
    if first:
        outs += [(own.shape, F32), (own.shape, F32), (own.shape[:2] + (128,), F32)]
    return call(functools.partial(update_body, first, len(recv)), operands, 1, outs)


def cells(rows, dim, seqs):
    across = seqs * 8 // rows
    return [(8 * (s // across), (s % across) * (dim // across)) for s in range(seqs)], dim // across


def deal_body(seqs, own_ref, *refs):
    out_ref = refs[-1]
    n, rows, dim = own_ref.shape
    spots, lanes = cells(rows, dim, seqs)
    for j in range(n):
        total = own_ref[j]
        for ref in refs[:-1]:
            total = total + ref[j].astype(F32)
        total = total.astype(BF)
        for s, (row, lane) in enumerate(spots):
            out_ref[s, j] = total[row : row + 8, lane : lane + lanes]


def deal(own, recv, seqs):
    n, rows, dim = own.shape
    shape = (seqs, n, 8, cells(rows, dim, seqs)[1])
    return call(functools.partial(deal_body, seqs), (own, *recv), 0, [(shape, BF)])[0]


def fold_body(got_ref, first_ref, second_ref, out_ref):
    seqs, n = got_ref.shape[:2]
    width = first_ref.shape[1]
    values = []
    for j in range(n):
        total = got_ref[0, j].astype(F32)
        for s in range(1, seqs):
            total = total + got_ref[s, j].astype(F32)
        values.append(total.astype(BF))
    level = jnp.zeros(got_ref.shape[2:], F32)
    pad = jnp.zeros((8, 128 - width), F32)
    level = jnp.concatenate([first_ref[...], pad, second_ref[...], pad], axis=1)
    high = level.astype(BF).astype(F32)
    mid = (level - high).astype(BF).astype(F32)
    low = level - high - mid
    line = lax.broadcasted_iota(jnp.int32, level.shape, 0)
    level = jnp.where(line == 0, high, jnp.where(line == 1, mid, low))
    values.append(level.astype(BF))
    for s in range(seqs):
        for j in range(n + 1):
            out_ref[s, j] = values[j]


def fold(got, first, second):
    seqs, n, rows, lanes = got.shape
    return call(fold_body, (got, first, second), 0, [((seqs, n + 1, rows, lanes), BF)])[0]


def finish_body(got_ref, gate_ref, up_ref, down_ref, level_ref):
    seqs, n = got_ref.shape[:2]
    rows, dim = down_ref.shape
    spots, lanes = cells(rows, dim, seqs)
    for j in range(n - 1):
        target = (gate_ref, up_ref, down_ref)[j]
        for s, (row, lane) in enumerate(spots):
            target[row : row + 8, lane : lane + lanes] = got_ref[s, j].astype(F32)
    best = None
    for s in range(seqs):
        terms = got_ref[s, n - 1].astype(F32)
        value = terms[0:1] + terms[1:2] + terms[2:3]
        best = value if best is None else jnp.maximum(best, value)
    level_ref[0:1, :] = best[:, :rows]
    level_ref[1:2, :] = best[:, 128 : 128 + rows]


def finish(got, rows, dim):
    outs = [((rows, dim), F32)] * 3 + [((2, rows), F32)]
    return call(finish_body, (got,), 0, outs)


def per_device(
    keys, values, queries, token_rate, valid_count, loss_scale, w_gate, w_up, w_down, out_cotangent
):
    parts = lax.axis_size("tok")
    seqs = lax.axis_size("seq")
    chips = parts // 2
    where = lax.axis_index("tok").reshape(1).astype(jnp.int32)

    def z_shift(array, k):
        pairs = [(2 * z + c, 2 * ((z + k) % chips) + c) for z in range(chips) for c in range(2)]
        return lax.ppermute(array, "tok", pairs)

    def other_core(array):
        return lax.ppermute(array, "tok", [(t, t ^ 1) for t in range(parts)])

    def scatter(own, other):
        sums = combine(own, other_core(other), chips)
        recv = []
        for k in range(1, chips):
            recv.append(z_shift(sums[k], k))
        return sums[0], recv

    def spread(piece):
        mine = [piece] + [z_shift(piece, chips - k) for k in range(1, chips)]
        return mine, [other_core(p) for p in mine]

    first, second = prep(where, w_gate, w_up, w_down, parts)
    half = w_gate.shape[1] // 2
    args = (where, valid_count, loss_scale, token_rate)

    def inner(block, halves):
        other = grads(True, block, args, keys, values, halves[1], BF)[0]
        own = grads(True, block, args, keys, values, halves[0], F32)[0]
        return scatter(own, other)

    own, recv = inner(0, ([first], [second]))
    piece, level0, *carried = update(loss_scale, own, recv, start=first)
    halves = spread(piece)
    acc, done = grads(False, 0, args, queries, out_cotangent, halves[0] + halves[1], F32, result=True)
    own, recv = inner(1, halves)
    piece, level1 = update(loss_scale, own, recv, carried=carried)
    halves = spread(piece)
    other = grads(False, 1, args, queries, out_cotangent, halves[1], BF, acc=acc, skip=half)[0]
    own = grads(False, 1, args, queries, out_cotangent, halves[0], F32, acc=acc, skip=0)[0]
    own, recv = scatter(own, other)
    fast_out = output_of(where, valid_count, queries, done, halves[0] + halves[1])
    dealt = lax.all_to_all(deal(own, recv, seqs), "seq", 0, 0)
    got = lax.all_to_all(fold(dealt, level0, level1), "seq", 0, 0)
    gate, up, down, level = finish(got, own.shape[1], own.shape[2])
    return (fast_out, gate.T, up.T, down, level)


def solution(mesh):
    placed = (
        P("seq", None, "tok", None),
        P("seq", None, "tok", None),
        P("seq", None, "tok", None),
        P("seq", None, "tok"),
        P("seq", None),
        P(),
        P(),
        P(),
        P(),
        P("seq", None, "tok", None),
    )

    return jax.shard_map(
        per_device,
        mesh=mesh,
        in_specs=placed,
        out_specs=(
            P("seq", None, "tok", None),
            P(None, "tok"),
            P(None, "tok"),
            P("tok", None),
            P(None, "tok"),
        ),
        check_vma=False,
    )
```

time: 367 us -> 134 us (0.37)
  waiting for transfers between devices: 243 us -> 38.6 us
  matrix products: 50.5 us -> 0 us
  starting transfers between devices: 0.52 us -> 35.4 us
  Pallas kernels: 0 us -> 27.7 us
  blocking collectives: 33.3 us -> 13.8 us
  between operations: 16.1 us -> 1.64 us
  other arithmetic: 11.8 us -> 0 us
    psum x3 -> x0, waiting for transfers between devices: 243 us -> none  [the longest x2 127 us: per_device(): summed = lax.psum((grads[0], grads[1], grads[2]), 'tok')]
    dot_general x26 -> x0, matrix products: 50.5 us -> none  [the longest x4 11.7 us: backward(): lax.dot_general(hidden, cotan, first, preferred_element_type=jnp.float32)]
    ppermute x0 -> x26, waiting for transfers between devices: none -> 38.6 us  [the longest x15 37.2 us: z_shift(): return lax.ppermute(array, 'tok', pairs)]
    pmax x1 -> x0, blocking collectives: 33.3 us -> none  [per_device(): level_list.append(lax.pmax(level_piece, 'seq'))]
    ppermute x0 -> x26, starting transfers between devices: none -> 31.9 us  [the longest x15 20.1 us: z_shift(): return lax.ppermute(array, 'tok', pairs)]
    pallas_call x0 -> x17, Pallas kernels: none -> 27.7 us  [call(): pl.pallas_call(body, in_specs=[SMEM] * n_smem + [VMEM] * (len(operands) -...]
    all_to_all x0 -> x1, blocking collectives: none -> 13.8 us  [per_device(): dealt = lax.all_to_all(deal(own, recv, seqs), 'seq', 0, 0)]
    unnamed x63 -> x58, local copies, waits for them, and re-layouts: 6.51 us -> 15.1 us
  transfers between devices with their start and end apart: 3 -> 27, of which waited for: 3 -> 13; matrix products, arithmetic and copies ran while one was open for 5% -> 0% of each run, Pallas kernels for 0% -> 13%
where the time goes in v2:
time: 134 us; the launch traced here: 132 us
  waiting for transfers between devices  38.6 us (29%)
  starting transfers between devices  35.4 us (26%)
  Pallas kernels  27.7 us (21%)
  local copies, waits for them, and re-layouts  15.1 us (11%)
  blocking collectives  13.8 us (10%)
  between operations  1.64 us (1%)
    ppermute x15, waiting for transfers between devices, z_shift(): return lax.ppermute(array, 'tok', pairs)  37.2 us
    pallas_call x17, Pallas kernels, call(): pl.pallas_call(body, in_specs=[SMEM] * n_smem + [VMEM] * (len(operands) -...  27.7 us
    ppermute x15, starting transfers between devices, z_shift(): return lax.ppermute(array, 'tok', pairs)  20.1 us
    unnamed x58, local copies, waits for them, and re-layouts  15.1 us
    all_to_all x1, blocking collectives, per_device(): dealt = lax.all_to_all(deal(own, recv, seqs), 'seq', 0, 0)  13.8 us
    ppermute x11, starting transfers between devices, other_core(): return lax.ppermute(array, 'tok', [(t, t ^ 1) for t in range(parts)])  11.8 us
    all_to_all x1, starting transfers between devices, per_device(): got = lax.all_to_all(fold(dealt, level0, level1), 'seq', 0, 0)  3.53 us
  transfers between devices with their start and end apart: 27, of which 13 were waited for; matrix products, arithmetic and copies ran while one was open for 0% of the time, Pallas kernels for 13%

profile of v2, /device:TPU:1, one launch (start us, length us, event | category | flops | bytes accessed | tf_op | source)
XLA Modules:
  0.0 132.3 jit_solution(16028717796666822534)
XLA Ops:
  4.8 1.6 %copy-done.1 = bf16[1,2,1024,512]{3,2,1,0:T(8,128)(2,1)S(1)} copy-done((bf16[1,2,1024,512]{3,2,1,0:T(8,128)(2,1)S(1)}, bf16[1,2,1024,512]{3,2,1,0:T(8,128)(2,1)}, u32[]{:S(2)}) %copy-start.1) | copy-done | bytes 2097176
  6.4 1.6 %copy-done.3 = bf16[1,2,1024,512]{3,2,1,0:T(8,128)(2,1)S(1)} copy-done((bf16[1,2,1024,512]{3,2,1,0:T(8,128)(2,1)S(1)}, bf16[1,2,1024,512]{3,2,1,0:T(8,128)(2,1)}, u32[]{:S(2)}) %copy-start.3) | copy-done | bytes 2097176
  9.3 2.7 %shard_map.139 = bf16[3,256,512]{2,1,0:T(8,128)(2,1)S(1)} custom-call(s32[1]{0:T(128)} %bitcast.where_ref, s32[1,2]{1,0:T(1,128)S(1)} %copy-done.27, f32[1]{0:T(128)S(6)} %copy.15.scale_ref, f32[1,2,1024]{2,1,0:T(2,128)S(1)} %copy-done.25, bf16[1,2,1024,512]{3,2,1,0:T(8,128)(2,1)S(1)} %copy-done.1, bf16[1,2,1024,512]{3,2,1,0:T(8,128)(2,1)S(1)} %copy-done.3, ...), custom_call_target="tpu_custom_call" | custom-call | flops 1610612736 | bytes 4194304 | tf_op jit(solution)/shard_map/pallas_call | solution.py:36
  12.0 1.5 %collective-permute-start = (bf16[3,256,512]{2,1,0:T(8,128)(2,1)S(1)}, bf16[3,256,512]{2,1,0:T(8,128)(2,1)S(1)}, u32[]{:S(2)}, u32[]{:S(2)}) collective-permute-start(bf16[3,256,512]{2,1,0:T(8,128)(2,1)S(1)} %shard_map.139), channel_id=1, source_target_pairs={{0,16},{16,0},{32,48},{48,32},{64,80},{80,64},{96,112},{112,96},{1... | collective-permute-start | bytes 2359304 | tf_op jit(solution)/shard_map/ppermute | solution.py:343
  13.5 2.6 %shard_map.138.own_ref = f32[3,256,512]{2,1,0:T(8,128)S(1)} custom-call(s32[1]{0:T(128)} %bitcast.where_ref, s32[1,2]{1,0:T(1,128)S(1)} %copy-done.27, f32[1]{0:T(128)S(6)} %copy.15.scale_ref, f32[1,2,1024]{2,1,0:T(2,128)S(1)} %copy-done.25, bf16[1,2,1024,512]{3,2,1,0:T(8,128)(2,1)S(1)} %copy-done.1, bf16[1,2,1024,512]{3,2,1,0:T(8,128)(2,1)S(1)} %copy-done.3, ...), custom_call_target="tpu_custom_call" | custom-call | flops 1610612736 | bytes 4194304 | tf_op jit(solution)/shard_map/pallas_call | solution.py:36
  16.3 1.8 %collective-permute-start.1 = (bf16[3,64,512]{2,1,0:T(8,128)(2,1)S(1)}, bf16[3,64,512]{2,1,0:T(8,128)(2,1)S(1)}, u32[]{:S(2)}, u32[]{:S(2)}) collective-permute-start(bf16[3,64,512]{2,1,0:T(8,128)(2,1)S(1)} %get-tuple-element.35), channel_id=1, source_target_pairs={{0,32},{16,48},{32,64},{48,80},{64,96},{80,112},{96,0},{112,16},{1... | collective-permute-start | bytes 589832 | tf_op jit(solution)/shard_map/ppermute | solution.py:340
  18.2 3.3 %collective-permute-start.2 = (bf16[3,64,512]{2,1,0:T(8,128)(2,1)S(1)}, bf16[3,64,512]{2,1,0:T(8,128)(2,1)S(1)}, u32[]{:S(2)}, u32[]{:S(2)}) collective-permute-start(bf16[3,64,512]{2,1,0:T(8,128)(2,1)S(1)} %get-tuple-element.36), channel_id=1, source_target_pairs={{0,64},{16,80},{32,96},{48,112},{64,0},{80,16},{96,32},{112,48},{1... | collective-permute-start | bytes 589832 | tf_op jit(solution)/shard_map/ppermute | solution.py:340
  22.2 3.3 %collective-permute-done.1.refs_0_ = bf16[3,64,512]{2,1,0:T(8,128)(2,1)S(1)} collective-permute-done((bf16[3,64,512]{2,1,0:T(8,128)(2,1)S(1)}, bf16[3,64,512]{2,1,0:T(8,128)(2,1)S(1)}, u32[]{:S(2)}, u32[]{:S(2)}) %collective-permute-start.1) | collective-permute-done | bytes 196640 | tf_op jit(solution)/shard_map/ppermute | solution.py:340
  25.5 5.1 %collective-permute-done.2.refs_1_ = bf16[3,64,512]{2,1,0:T(8,128)(2,1)S(1)} collective-permute-done((bf16[3,64,512]{2,1,0:T(8,128)(2,1)S(1)}, bf16[3,64,512]{2,1,0:T(8,128)(2,1)S(1)}, u32[]{:S(2)}, u32[]{:S(2)}) %collective-permute-start.2) | collective-permute-done | bytes 196640 | tf_op jit(solution)/shard_map/ppermute | solution.py:340
  32.0 2.5 %collective-permute-start.5 = (bf16[1,3,64,512]{3,2,1,0:T(8,128)(2,1)S(1)}, bf16[1,3,64,512]{3,2,1,0:T(8,128)(2,1)S(1)}, u32[]{:S(2)}, u32[]{:S(2)}) collective-permute-start(bf16[1,3,64,512]{3,2,1,0:T(8,128)(2,1)S(1)} %get-tuple-element.38.refs_0_), channel_id=1, source_target_pairs={{0,64},{16,80},{32,96},{48,112},{64,0},{80,16},{96,32},{112,48},{1... | collective-permute-start | bytes 589832 | tf_op jit(solution)/shard_map/ppermute | solution.py:340
  34.8 2.0 %collective-permute-start.7 = (bf16[1,3,64,512]{3,2,1,0:T(8,128)(2,1)S(1)}, bf16[1,3,64,512]{3,2,1,0:T(8,128)(2,1)S(1)}, u32[]{:S(2)}, u32[]{:S(2)}) collective-permute-start(bf16[1,3,64,512]{3,2,1,0:T(8,128)(2,1)S(1)} %get-tuple-element.38.refs_0_), channel_id=1, source_target_pairs={{0,16},{16,0},{32,48},{48,32},{64,80},{80,64},{96,112},{112,96},{1... | collective-permute-start | bytes 589832 | tf_op jit(solution)/shard_map/ppermute | solution.py:343
  37.8 1.9 %collective-permute-start.10 = (bf16[1,3,64,512]{3,2,1,0:T(8,128)(2,1)S(1)}, bf16[1,3,64,512]{3,2,1,0:T(8,128)(2,1)S(1)}, u32[]{:S(2)}, u32[]{:S(2)}) collective-permute-start(bf16[1,3,64,512]{3,2,1,0:T(8,128)(2,1)S(1)} %collective-permute-done.6.refs_3_), channel_id=1, source_target_pairs={{0,16},{16,0},{32,48},{48,32},{64,80},{80,64},{96,112},{112,96},{1... | collective-permute-start | bytes 589832 | tf_op jit(solution)/shard_map/ppermute | solution.py:343
  39.7 3.4 %collective-permute-done.5.refs_2_ = bf16[1,3,64,512]{3,2,1,0:T(8,128)(2,1)S(1)} collective-permute-done((bf16[1,3,64,512]{3,2,1,0:T(8,128)(2,1)S(1)}, bf16[1,3,64,512]{3,2,1,0:T(8,128)(2,1)S(1)}, u32[]{:S(2)}, u32[]{:S(2)}) %collective-permute-start.5) | collective-permute-done | bytes 196640 | tf_op jit(solution)/shard_map/ppermute | solution.py:340
  43.2 1.3 %collective-permute-start.9 = (bf16[1,3,64,512]{3,2,1,0:T(8,128)(2,1)S(1)}, bf16[1,3,64,512]{3,2,1,0:T(8,128)(2,1)S(1)}, u32[]{:S(2)}, u32[]{:S(2)}) collective-permute-start(bf16[1,3,64,512]{3,2,1,0:T(8,128)(2,1)S(1)} %collective-permute-done.5.refs_2_), channel_id=1, source_target_pairs={{0,16},{16,0},{32,48},{48,32},{64,80},{80,64},{96,112},{112,96},{1... | collective-permute-start | bytes 589832 | tf_op jit(solution)/shard_map/ppermute | solution.py:343
  46.0 2.6 %shard_map.144 = bf16[3,256,512]{2,1,0:T(8,128)(2,1)S(1)} custom-call(s32[1]{0:T(128)} %bitcast.where_ref, s32[1,2]{1,0:T(1,128)S(1)} %copy-done.28, f32[1]{0:T(128)S(6)} %copy.15.scale_ref, f32[1,2,1024]{2,1,0:T(2,128)S(1)} %copy-done.26, bf16[1,2,1024,512]{3,2,1,0:T(8,128)(2,1)S(1)} %copy-done.2, bf16[1,2,1024,512]{3,2,1,0:T(8,128)(2,1)S(1)} %copy-done.4, ...), custom_call_target="tpu_custom_call" | custom-call | flops 1610612736 | bytes 4194304 | tf_op jit(solution)/shard_map/pallas_call | solution.py:36
  49.0 2.6 %shard_map.143.own_ref = f32[3,256,512]{2,1,0:T(8,128)S(1)} custom-call(s32[1]{0:T(128)} %bitcast.where_ref, s32[1,2]{1,0:T(1,128)S(1)} %copy-done.28, f32[1]{0:T(128)S(6)} %copy.15.scale_ref, f32[1,2,1024]{2,1,0:T(2,128)S(1)} %copy-done.26, bf16[1,2,1024,512]{3,2,1,0:T(8,128)(2,1)S(1)} %copy-done.2, bf16[1,2,1024,512]{3,2,1,0:T(8,128)(2,1)S(1)} %copy-done.4, ...), custom_call_target="tpu_custom_call" | custom-call | flops 1610612736 | bytes 4194304 | tf_op jit(solution)/shard_map/pallas_call | solution.py:36
  52.5 2.5 %collective-permute-start.13 = (bf16[3,64,512]{2,1,0:T(8,128)(2,1)S(1)}, bf16[3,64,512]{2,1,0:T(8,128)(2,1)S(1)}, u32[]{:S(2)}, u32[]{:S(2)}) collective-permute-start(bf16[3,64,512]{2,1,0:T(8,128)(2,1)S(1)} %get-tuple-element.42), channel_id=1, source_target_pairs={{0,64},{16,80},{32,96},{48,112},{64,0},{80,16},{96,32},{112,48},{1... | collective-permute-start | bytes 589832 | tf_op jit(solution)/shard_map/ppermute | solution.py:340
  55.2 4.1 %collective-permute-done.12.refs_0_ = bf16[3,64,512]{2,1,0:T(8,128)(2,1)S(1)} collective-permute-done((bf16[3,64,512]{2,1,0:T(8,128)(2,1)S(1)}, bf16[3,64,512]{2,1,0:T(8,128)(2,1)S(1)}, u32[]{:S(2)}, u32[]{:S(2)}) %collective-permute-start.12) | collective-permute-done | bytes 196640 | tf_op jit(solution)/shard_map/ppermute | solution.py:340
  59.3 4.8 %collective-permute-done.13.refs_1_ = bf16[3,64,512]{2,1,0:T(8,128)(2,1)S(1)} collective-permute-done((bf16[3,64,512]{2,1,0:T(8,128)(2,1)S(1)}, bf16[3,64,512]{2,1,0:T(8,128)(2,1)S(1)}, u32[]{:S(2)}, u32[]{:S(2)}) %collective-permute-start.13) | collective-permute-done | bytes 196640 | tf_op jit(solution)/shard_map/ppermute | solution.py:340
  65.8 2.9 %collective-permute-start.16 = (bf16[1,3,64,512]{3,2,1,0:T(8,128)(2,1)S(1)}, bf16[1,3,64,512]{3,2,1,0:T(8,128)(2,1)S(1)}, u32[]{:S(2)}, u32[]{:S(2)}) collective-permute-start(bf16[1,3,64,512]{3,2,1,0:T(8,128)(2,1)S(1)} %get-tuple-element.47.refs_0_), channel_id=1, source_target_pairs={{0,64},{16,80},{32,96},{48,112},{64,0},{80,16},{96,32},{112,48},{1... | collective-permute-start | bytes 589832 | tf_op jit(solution)/shard_map/ppermute | solution.py:340
  69.8 1.9 %collective-permute-done.17.refs_3_ = bf16[1,3,64,512]{3,2,1,0:T(8,128)(2,1)S(1)} collective-permute-done((bf16[1,3,64,512]{3,2,1,0:T(8,128)(2,1)S(1)}, bf16[1,3,64,512]{3,2,1,0:T(8,128)(2,1)S(1)}, u32[]{:S(2)}, u32[]{:S(2)}) %collective-permute-start.17) | collective-permute-done | bytes 196640 | tf_op jit(solution)/shard_map/ppermute | solution.py:340
  71.7 1.7 %collective-permute-start.21 = (bf16[1,3,64,512]{3,2,1,0:T(8,128)(2,1)S(1)}, bf16[1,3,64,512]{3,2,1,0:T(8,128)(2,1)S(1)}, u32[]{:S(2)}, u32[]{:S(2)}) collective-permute-start(bf16[1,3,64,512]{3,2,1,0:T(8,128)(2,1)S(1)} %collective-permute-done.17.refs_3_), channel_id=1, source_target_pairs={{0,16},{16,0},{32,48},{48,32},{64,80},{80,64},{96,112},{112,96},{1... | collective-permute-start | bytes 589832 | tf_op jit(solution)/shard_map/ppermute | solution.py:343
  73.4 4.0 %collective-permute-done.16.refs_2_ = bf16[1,3,64,512]{3,2,1,0:T(8,128)(2,1)S(1)} collective-permute-done((bf16[1,3,64,512]{3,2,1,0:T(8,128)(2,1)S(1)}, bf16[1,3,64,512]{3,2,1,0:T(8,128)(2,1)S(1)}, u32[]{:S(2)}, u32[]{:S(2)}) %collective-permute-start.16) | collective-permute-done | bytes 196640 | tf_op jit(solution)/shard_map/ppermute | solution.py:340
  78.9 4.9 %shard_map.142 = (f32[3,512,512]{2,1,0:T(8,128)S(1)}, bf16[1024,512]{1,0:T(8,128)(2,1)S(1)}) custom-call(s32[1]{0:T(128)} %bitcast.where_ref, s32[1,2]{1,0:T(1,128)S(1)} %copy-done.28, f32[1]{0:T(128)S(6)} %copy.15.scale_ref, f32[1,2,1024]{2,1,0:T(2,128)S(1)} %copy-done.26, bf16[1,2,1024,512]{3,2,1,0:T(8,128)(2,1)S(1)} %copy-done, ...), custom_call_target="tpu_custom_call" | custom-call | flops 3221225472 | bytes 4194304 | tf_op jit(solution)/shard_map/pallas_call | solution.py:36
  83.8 2.6 %shard_map.149 = bf16[3,256,512]{2,1,0:T(8,128)(2,1)S(1)} custom-call(s32[1]{0:T(128)} %bitcast.where_ref, s32[1,2]{1,0:T(1,128)S(1)} %copy-done.28, f32[1]{0:T(128)S(6)} %copy.15.scale_ref, f32[1,2,1024]{2,1,0:T(2,128)S(1)} %copy-done.26, bf16[1,2,1024,512]{3,2,1,0:T(8,128)(2,1)S(1)} %copy-done, bf16[1,2,1024,512]{3,2,1,0:T(8,128)(2,1)S(1)} %copy-done.5, ...), custom_call_target="tpu_custom_call" | custom-call | flops 1610612736 | bytes 4194304 | tf_op jit(solution)/shard_map/pallas_call | solution.py:36
  87.0 2.6 %shard_map.148.own_ref = f32[3,256,512]{2,1,0:T(8,128)S(1)} custom-call(s32[1]{0:T(128)} %bitcast.where_ref, s32[1,2]{1,0:T(1,128)S(1)} %copy-done.28, f32[1]{0:T(128)S(6)} %copy.15.scale_ref, f32[1,2,1024]{2,1,0:T(2,128)S(1)} %copy-done.26, bf16[1,2,1024,512]{3,2,1,0:T(8,128)(2,1)S(1)} %copy-done, bf16[1,2,1024,512]{3,2,1,0:T(8,128)(2,1)S(1)} %copy-done.5, ...), custom_call_target="tpu_custom_call" | custom-call | flops 1610612736 | bytes 4194304 | tf_op jit(solution)/shard_map/pallas_call | solution.py:36
  89.8 2.6 %collective-permute-start.24 = (bf16[3,64,512]{2,1,0:T(8,128)(2,1)S(1)}, bf16[3,64,512]{2,1,0:T(8,128)(2,1)S(1)}, u32[]{:S(2)}, u32[]{:S(2)}) collective-permute-start(bf16[3,64,512]{2,1,0:T(8,128)(2,1)S(1)} %get-tuple-element.51), channel_id=1, source_target_pairs={{0,64},{16,80},{32,96},{48,112},{64,0},{80,16},{96,32},{112,48},{1... | collective-permute-start | bytes 589832 | tf_op jit(solution)/shard_map/ppermute | solution.py:340
  92.5 5.3 %collective-permute-done.23.refs_0_ = bf16[3,64,512]{2,1,0:T(8,128)(2,1)S(1)} collective-permute-done((bf16[3,64,512]{2,1,0:T(8,128)(2,1)S(1)}, bf16[3,64,512]{2,1,0:T(8,128)(2,1)S(1)}, u32[]{:S(2)}, u32[]{:S(2)}) %collective-permute-start.23) | collective-permute-done | bytes 196640 | tf_op jit(solution)/shard_map/ppermute | solution.py:340
  97.9 3.3 %collective-permute-done.24.refs_1_ = bf16[3,64,512]{2,1,0:T(8,128)(2,1)S(1)} collective-permute-done((bf16[3,64,512]{2,1,0:T(8,128)(2,1)S(1)}, bf16[3,64,512]{2,1,0:T(8,128)(2,1)S(1)}, u32[]{:S(2)}, u32[]{:S(2)}) %collective-permute-start.24) | collective-permute-done | bytes 196640 | tf_op jit(solution)/shard_map/ppermute | solution.py:340
  102.0 13.8 %all_to_all.10.got_ref = bf16[16,3,8,256]{3,2,1,0:T(8,128)(2,1)S(1)} all-to-all(bf16[16,3,8,256]{3,2,1,0:T(8,128)(2,1)S(1)} %shard_map.151), channel_id=1, replica_groups=mesh['tok'=8,'seq'=16] {'seq'}, dimensions={0} | all-to-all | bytes 393216 | tf_op jit(solution)/shard_map/all_to_all | solution.py:376
  116.6 3.5 %all-to-all-start.1 = ((bf16[16,4,8,256]{3,2,1,0:T(8,128)(2,1)}), bf16[16,4,8,256]{3,2,1,0:T(8,128)(2,1)S(1)}, u32[]{:S(2)}, u32[]{:S(2)}) async-start(bf16[16,4,8,256]{3,2,1,0:T(8,128)(2,1)} %shard_map.152), calls=%async_computation.1 | async-start | bytes 524288 | tf_op jit(solution)/shard_map/all_to_all | solution.py:377
  127.6 4.0 %shard_map.147 = bf16[1,2,1024,512]{3,2,1,0:T(8,128)(2,1)} custom-call(s32[1]{0:T(128)} %bitcast.where_ref, s32[1,2]{1,0:T(1,128)S(1)} %copy-done.28, bf16[1,2,1024,512]{3,2,1,0:T(8,128)(2,1)S(1)} %copy-done, bf16[1024,512]{1,0:T(8,128)(2,1)S(1)} %get-tuple-element.39.done_ref, bf16[1,3,64,512]{3,2,1,0:T(8,128)(2,1)S(1)} %copy-done.7, ...), custom_call_target="tpu_custom_call" | custom-call | flops 1610612736 | bytes 4194304 | tf_op jit(solution)/shard_map/pallas_call | solution.py:36
  (98 shorter events, 26.2 us)
Async XLA Ops:
  12.0 4.1 %collective-permute-start = (bf16[3,256,512]{2,1,0:T(8,128)(2,1)S(1)}, bf16[3,256,512]{2,1,0:T(8,128)(2,1)S(1)}, u32[]{:S(2)}, u32[]{:S(2)}) collective-permute-start(bf16[3,256,512]{2,1,0:T(8,128)(2,1)S(1)} %shard_map.139), channel_id=1, source_target_pairs={{0,16},{16,0},{32,48},{48,32},{64,80},{80,64},{96,112},{112,96},{1... | collective-permute-start | bytes 2359304 | tf_op jit(solution)/shard_map/ppermute | solution.py:343
  13.5 32.5 %copy-start.4 = (bf16[1,2,1024,512]{3,2,1,0:T(8,128)(2,1)S(1)}, bf16[1,2,1024,512]{3,2,1,0:T(8,128)(2,1)}, u32[]{:S(2)}) copy-start(bf16[1,2,1024,512]{3,2,1,0:T(8,128)(2,1)} %e_ref.11) | copy-start | bytes 6291460
  16.1 29.9 %copy-start.2 = (bf16[1,2,1024,512]{3,2,1,0:T(8,128)(2,1)S(1)}, bf16[1,2,1024,512]{3,2,1,0:T(8,128)(2,1)}, u32[]{:S(2)}) copy-start(bf16[1,2,1024,512]{3,2,1,0:T(8,128)(2,1)} %x_ref.12) | copy-start | bytes 6291460
  16.1 29.9 %copy-start.26 = (f32[1,2,1024]{2,1,0:T(2,128)S(1)}, f32[1,2,1024]{2,1,0:T(2,128)}, u32[]{:S(2)}) copy-start(f32[1,2,1024]{2,1,0:T(2,128)} %rate_ref.13) | copy-start | bytes 24580
  16.1 29.9 %copy-start.28 = (s32[1,2]{1,0:T(1,128)S(1)}, s32[1,2]{1,0:T(1,128)}, u32[]{:S(2)}) copy-start(s32[1,2]{1,0:T(1,128)} %count_ref.15) | copy-start | bytes 28
  16.3 9.2 %collective-permute-start.1 = (bf16[3,64,512]{2,1,0:T(8,128)(2,1)S(1)}, bf16[3,64,512]{2,1,0:T(8,128)(2,1)S(1)}, u32[]{:S(2)}, u32[]{:S(2)}) collective-permute-start(bf16[3,64,512]{2,1,0:T(8,128)(2,1)S(1)} %get-tuple-element.35), channel_id=1, source_target_pairs={{0,32},{16,48},{32,64},{48,80},{64,96},{80,112},{96,0},{112,16},{1... | collective-permute-start | bytes 589832 | tf_op jit(solution)/shard_map/ppermute | solution.py:340
  18.2 12.5 %collective-permute-start.2 = (bf16[3,64,512]{2,1,0:T(8,128)(2,1)S(1)}, bf16[3,64,512]{2,1,0:T(8,128)(2,1)S(1)}, u32[]{:S(2)}, u32[]{:S(2)}) collective-permute-start(bf16[3,64,512]{2,1,0:T(8,128)(2,1)S(1)} %get-tuple-element.36), channel_id=1, source_target_pairs={{0,64},{16,80},{32,96},{48,112},{64,0},{80,16},{96,32},{112,48},{1... | collective-permute-start | bytes 589832 | tf_op jit(solution)/shard_map/ppermute | solution.py:340
  21.5 9.2 %collective-permute-start.3 = (bf16[3,64,512]{2,1,0:T(8,128)(2,1)S(1)}, bf16[3,64,512]{2,1,0:T(8,128)(2,1)S(1)}, u32[]{:S(2)}, u32[]{:S(2)}) collective-permute-start(bf16[3,64,512]{2,1,0:T(8,128)(2,1)S(1)} %get-tuple-element.37), channel_id=1, source_target_pairs={{0,96},{16,112},{32,0},{48,16},{64,32},{80,48},{96,64},{112,80},{1... | collective-permute-start | bytes 589832 | tf_op jit(solution)/shard_map/ppermute | solution.py:340
  31.0 6.9 %collective-permute-start.6 = (bf16[1,3,64,512]{3,2,1,0:T(8,128)(2,1)S(1)}, bf16[1,3,64,512]{3,2,1,0:T(8,128)(2,1)S(1)}, u32[]{:S(2)}, u32[]{:S(2)}) collective-permute-start(bf16[1,3,64,512]{3,2,1,0:T(8,128)(2,1)S(1)} %get-tuple-element.38.refs_0_), channel_id=1, source_target_pairs={{0,32},{16,48},{32,64},{48,80},{64,96},{80,112},{96,0},{112,16},{1... | collective-permute-start | bytes 589832 | tf_op jit(solution)/shard_map/ppermute | solution.py:340
  32.0 11.2 %collective-permute-start.5 = (bf16[1,3,64,512]{3,2,1,0:T(8,128)(2,1)S(1)}, bf16[1,3,64,512]{3,2,1,0:T(8,128)(2,1)S(1)}, u32[]{:S(2)}, u32[]{:S(2)}) collective-permute-start(bf16[1,3,64,512]{3,2,1,0:T(8,128)(2,1)S(1)} %get-tuple-element.38.refs_0_), channel_id=1, source_target_pairs={{0,64},{16,80},{32,96},{48,112},{64,0},{80,16},{96,32},{112,48},{1... | collective-permute-start | bytes 589832 | tf_op jit(solution)/shard_map/ppermute | solution.py:340
  34.5 10.1 %collective-permute-start.4 = (bf16[1,3,64,512]{3,2,1,0:T(8,128)(2,1)S(1)}, bf16[1,3,64,512]{3,2,1,0:T(8,128)(2,1)S(1)}, u32[]{:S(2)}, u32[]{:S(2)}) collective-permute-start(bf16[1,3,64,512]{3,2,1,0:T(8,128)(2,1)S(1)} %get-tuple-element.38.refs_0_), channel_id=1, source_target_pairs={{0,96},{16,112},{32,0},{48,16},{64,32},{80,48},{96,64},{112,80},{1... | collective-permute-start | bytes 589832 | tf_op jit(solution)/shard_map/ppermute | solution.py:340
  34.8 9.8 %collective-permute-start.7 = (bf16[1,3,64,512]{3,2,1,0:T(8,128)(2,1)S(1)}, bf16[1,3,64,512]{3,2,1,0:T(8,128)(2,1)S(1)}, u32[]{:S(2)}, u32[]{:S(2)}) collective-permute-start(bf16[1,3,64,512]{3,2,1,0:T(8,128)(2,1)S(1)} %get-tuple-element.38.refs_0_), channel_id=1, source_target_pairs={{0,16},{16,0},{32,48},{48,32},{64,80},{80,64},{96,112},{112,96},{1... | collective-permute-start | bytes 589832 | tf_op jit(solution)/shard_map/ppermute | solution.py:343
  37.8 6.7 %collective-permute-start.10 = (bf16[1,3,64,512]{3,2,1,0:T(8,128)(2,1)S(1)}, bf16[1,3,64,512]{3,2,1,0:T(8,128)(2,1)S(1)}, u32[]{:S(2)}, u32[]{:S(2)}) collective-permute-start(bf16[1,3,64,512]{3,2,1,0:T(8,128)(2,1)S(1)} %collective-permute-done.6.refs_3_), channel_id=1, source_target_pairs={{0,16},{16,0},{32,48},{48,32},{64,80},{80,64},{96,112},{112,96},{1... | collective-permute-start | bytes 589832 | tf_op jit(solution)/shard_map/ppermute | solution.py:343
  43.2 2.4 %collective-permute-start.9 = (bf16[1,3,64,512]{3,2,1,0:T(8,128)(2,1)S(1)}, bf16[1,3,64,512]{3,2,1,0:T(8,128)(2,1)S(1)}, u32[]{:S(2)}, u32[]{:S(2)}) collective-permute-start(bf16[1,3,64,512]{3,2,1,0:T(8,128)(2,1)S(1)} %collective-permute-done.5.refs_2_), channel_id=1, source_target_pairs={{0,16},{16,0},{32,48},{48,32},{64,80},{80,64},{96,112},{112,96},{1... | collective-permute-start | bytes 589832 | tf_op jit(solution)/shard_map/ppermute | solution.py:343
  44.5 1.4 %collective-permute-start.8 = (bf16[1,3,64,512]{3,2,1,0:T(8,128)(2,1)S(1)}, bf16[1,3,64,512]{3,2,1,0:T(8,128)(2,1)S(1)}, u32[]{:S(2)}, u32[]{:S(2)}) collective-permute-start(bf16[1,3,64,512]{3,2,1,0:T(8,128)(2,1)S(1)} %collective-permute-done.4.refs_1_), channel_id=1, source_target_pairs={{0,16},{16,0},{32,48},{48,32},{64,80},{80,64},{96,112},{112,96},{1... | collective-permute-start | bytes 589832 | tf_op jit(solution)/shard_map/ppermute | solution.py:343
  48.6 3.0 %collective-permute-start.11 = (bf16[3,256,512]{2,1,0:T(8,128)(2,1)S(1)}, bf16[3,256,512]{2,1,0:T(8,128)(2,1)S(1)}, u32[]{:S(2)}, u32[]{:S(2)}) collective-permute-start(bf16[3,256,512]{2,1,0:T(8,128)(2,1)S(1)} %shard_map.144), channel_id=1, source_target_pairs={{0,16},{16,0},{32,48},{48,32},{64,80},{80,64},{96,112},{112,96},{1... | collective-permute-start | bytes 2359304 | tf_op jit(solution)/shard_map/ppermute | solution.py:343
  51.6 27.2 %copy-start = (bf16[1,2,1024,512]{3,2,1,0:T(8,128)(2,1)S(1)}, bf16[1,2,1024,512]{3,2,1,0:T(8,128)(2,1)}, u32[]{:S(2)}) copy-start(bf16[1,2,1024,512]{3,2,1,0:T(8,128)(2,1)} %x_ref.15) | copy-start | bytes 6291460
  51.8 7.5 %collective-permute-start.12 = (bf16[3,64,512]{2,1,0:T(8,128)(2,1)S(1)}, bf16[3,64,512]{2,1,0:T(8,128)(2,1)S(1)}, u32[]{:S(2)}, u32[]{:S(2)}) collective-permute-start(bf16[3,64,512]{2,1,0:T(8,128)(2,1)S(1)} %get-tuple-element.41), channel_id=1, source_target_pairs={{0,32},{16,48},{32,64},{48,80},{64,96},{80,112},{96,0},{112,16},{1... | collective-permute-start | bytes 589832 | tf_op jit(solution)/shard_map/ppermute | solution.py:340
  52.5 11.6 %collective-permute-start.13 = (bf16[3,64,512]{2,1,0:T(8,128)(2,1)S(1)}, bf16[3,64,512]{2,1,0:T(8,128)(2,1)S(1)}, u32[]{:S(2)}, u32[]{:S(2)}) collective-permute-start(bf16[3,64,512]{2,1,0:T(8,128)(2,1)S(1)} %get-tuple-element.42), channel_id=1, source_target_pairs={{0,64},{16,80},{32,96},{48,112},{64,0},{80,16},{96,32},{112,48},{1... | collective-permute-start | bytes 589832 | tf_op jit(solution)/shard_map/ppermute | solution.py:340
  55.0 9.1 %collective-permute-start.14 = (bf16[3,64,512]{2,1,0:T(8,128)(2,1)S(1)}, bf16[3,64,512]{2,1,0:T(8,128)(2,1)S(1)}, u32[]{:S(2)}, u32[]{:S(2)}) collective-permute-start(bf16[3,64,512]{2,1,0:T(8,128)(2,1)S(1)} %get-tuple-element.43), channel_id=1, source_target_pairs={{0,96},{16,112},{32,0},{48,16},{64,32},{80,48},{96,64},{112,80},{1... | collective-permute-start | bytes 589832 | tf_op jit(solution)/shard_map/ppermute | solution.py:340
  64.4 7.3 %collective-permute-start.17 = (bf16[1,3,64,512]{3,2,1,0:T(8,128)(2,1)S(1)}, bf16[1,3,64,512]{3,2,1,0:T(8,128)(2,1)S(1)}, u32[]{:S(2)}, u32[]{:S(2)}) collective-permute-start(bf16[1,3,64,512]{3,2,1,0:T(8,128)(2,1)S(1)} %get-tuple-element.47.refs_0_), channel_id=1, source_target_pairs={{0,32},{16,48},{32,64},{48,80},{64,96},{80,112},{96,0},{112,16},{1... | collective-permute-start | bytes 589832 | tf_op jit(solution)/shard_map/ppermute | solution.py:340
  65.8 11.6 %collective-permute-start.16 = (bf16[1,3,64,512]{3,2,1,0:T(8,128)(2,1)S(1)}, bf16[1,3,64,512]{3,2,1,0:T(8,128)(2,1)S(1)}, u32[]{:S(2)}, u32[]{:S(2)}) collective-permute-start(bf16[1,3,64,512]{3,2,1,0:T(8,128)(2,1)S(1)} %get-tuple-element.47.refs_0_), channel_id=1, source_target_pairs={{0,64},{16,80},{32,96},{48,112},{64,0},{80,16},{96,32},{112,48},{1... | collective-permute-start | bytes 589832 | tf_op jit(solution)/shard_map/ppermute | solution.py:340
  68.7 10.1 %collective-permute-start.15 = (bf16[1,3,64,512]{3,2,1,0:T(8,128)(2,1)S(1)}, bf16[1,3,64,512]{3,2,1,0:T(8,128)(2,1)S(1)}, u32[]{:S(2)}, u32[]{:S(2)}) collective-permute-start(bf16[1,3,64,512]{3,2,1,0:T(8,128)(2,1)S(1)} %get-tuple-element.47.refs_0_), channel_id=1, source_target_pairs={{0,96},{16,112},{32,0},{48,16},{64,32},{80,48},{96,64},{112,80},{1... | collective-permute-start | bytes 589832 | tf_op jit(solution)/shard_map/ppermute | solution.py:340
  68.7 15.0 %collective-permute-start.18 = (bf16[1,3,64,512]{3,2,1,0:T(8,128)(2,1)S(1)}, bf16[1,3,64,512]{3,2,1,0:T(8,128)(2,1)S(1)}, u32[]{:S(2)}, u32[]{:S(2)}) collective-permute-start(bf16[1,3,64,512]{3,2,1,0:T(8,128)(2,1)S(1)} %get-tuple-element.47.refs_0_), channel_id=1, source_target_pairs={{0,16},{16,0},{32,48},{48,32},{64,80},{80,64},{96,112},{112,96},{1... | collective-permute-start | bytes 589832 | tf_op jit(solution)/shard_map/ppermute | solution.py:343
  71.7 12.1 %collective-permute-start.21 = (bf16[1,3,64,512]{3,2,1,0:T(8,128)(2,1)S(1)}, bf16[1,3,64,512]{3,2,1,0:T(8,128)(2,1)S(1)}, u32[]{:S(2)}, u32[]{:S(2)}) collective-permute-start(bf16[1,3,64,512]{3,2,1,0:T(8,128)(2,1)S(1)} %collective-permute-done.17.refs_3_), channel_id=1, source_target_pairs={{0,16},{16,0},{32,48},{48,32},{64,80},{80,64},{96,112},{112,96},{1... | collective-permute-start | bytes 589832 | tf_op jit(solution)/shard_map/ppermute | solution.py:343
  77.4 6.4 %collective-permute-start.20 = (bf16[1,3,64,512]{3,2,1,0:T(8,128)(2,1)S(1)}, bf16[1,3,64,512]{3,2,1,0:T(8,128)(2,1)S(1)}, u32[]{:S(2)}, u32[]{:S(2)}) collective-permute-start(bf16[1,3,64,512]{3,2,1,0:T(8,128)(2,1)S(1)} %collective-permute-done.16.refs_2_), channel_id=1, source_target_pairs={{0,16},{16,0},{32,48},{48,32},{64,80},{80,64},{96,112},{112,96},{1... | collective-permute-start | bytes 589832 | tf_op jit(solution)/shard_map/ppermute | solution.py:343
  78.8 5.0 %collective-permute-start.19 = (bf16[1,3,64,512]{3,2,1,0:T(8,128)(2,1)S(1)}, bf16[1,3,64,512]{3,2,1,0:T(8,128)(2,1)S(1)}, u32[]{:S(2)}, u32[]{:S(2)}) collective-permute-start(bf16[1,3,64,512]{3,2,1,0:T(8,128)(2,1)S(1)} %collective-permute-done.15.refs_1_), channel_id=1, source_target_pairs={{0,16},{16,0},{32,48},{48,32},{64,80},{80,64},{96,112},{112,96},{1... | collective-permute-start | bytes 589832 | tf_op jit(solution)/shard_map/ppermute | solution.py:343
  86.5 3.1 %collective-permute-start.22 = (bf16[3,256,512]{2,1,0:T(8,128)(2,1)S(1)}, bf16[3,256,512]{2,1,0:T(8,128)(2,1)S(1)}, u32[]{:S(2)}, u32[]{:S(2)}) collective-permute-start(bf16[3,256,512]{2,1,0:T(8,128)(2,1)S(1)} %shard_map.149), channel_id=1, source_target_pairs={{0,16},{16,0},{32,48},{48,32},{64,80},{80,64},{96,112},{112,96},{1... | collective-permute-start | bytes 2359304 | tf_op jit(solution)/shard_map/ppermute | solution.py:343
  89.8 8.1 %collective-permute-start.23 = (bf16[3,64,512]{2,1,0:T(8,128)(2,1)S(1)}, bf16[3,64,512]{2,1,0:T(8,128)(2,1)S(1)}, u32[]{:S(2)}, u32[]{:S(2)}) collective-permute-start(bf16[3,64,512]{2,1,0:T(8,128)(2,1)S(1)} %get-tuple-element.50), channel_id=1, source_target_pairs={{0,32},{16,48},{32,64},{48,80},{64,96},{80,112},{96,0},{112,16},{1... | collective-permute-start | bytes 589832 | tf_op jit(solution)/shard_map/ppermute | solution.py:340
  89.8 11.3 %collective-permute-start.24 = (bf16[3,64,512]{2,1,0:T(8,128)(2,1)S(1)}, bf16[3,64,512]{2,1,0:T(8,128)(2,1)S(1)}, u32[]{:S(2)}, u32[]{:S(2)}) collective-permute-start(bf16[3,64,512]{2,1,0:T(8,128)(2,1)S(1)} %get-tuple-element.51), channel_id=1, source_target_pairs={{0,64},{16,80},{32,96},{48,112},{64,0},{80,16},{96,32},{112,48},{1... | collective-permute-start | bytes 589832 | tf_op jit(solution)/shard_map/ppermute | solution.py:340
  92.4 9.5 %collective-permute-start.25 = (bf16[3,64,512]{2,1,0:T(8,128)(2,1)S(1)}, bf16[3,64,512]{2,1,0:T(8,128)(2,1)S(1)}, u32[]{:S(2)}, u32[]{:S(2)}) collective-permute-start(bf16[3,64,512]{2,1,0:T(8,128)(2,1)S(1)} %get-tuple-element.52), channel_id=1, source_target_pairs={{0,96},{16,112},{32,0},{48,16},{64,32},{80,48},{96,64},{112,80},{1... | collective-permute-start | bytes 589832 | tf_op jit(solution)/shard_map/ppermute | solution.py:340
  116.6 14.9 %all-to-all-start.1 = ((bf16[16,4,8,256]{3,2,1,0:T(8,128)(2,1)}), bf16[16,4,8,256]{3,2,1,0:T(8,128)(2,1)S(1)}, u32[]{:S(2)}, u32[]{:S(2)}) async-start(bf16[16,4,8,256]{3,2,1,0:T(8,128)(2,1)} %shard_map.152), calls=%async_computation.1 | async-start | bytes 524288 | tf_op jit(solution)/shard_map/all_to_all | solution.py:377
  (24 other events, 108.6 us)

commit v3 on v2

v3 whole, which is shorter than its diff:
```python
import functools
import math
import jax
import jax.numpy as jnp
from jax import lax
from jax.experimental import pallas as pl
from jax.experimental.pallas import tpu as pltpu
from jax.sharding import PartitionSpec as P


KEEP = 0.9
RATE = 3.0
TINY = 1e-06
BF = jnp.bfloat16
F32 = jnp.float32
NT = (((1,), (1,)), ((), ()))
TN = (((0,), (0,)), ((), ()))
MIB = 1024 * 1024
TILE = 512


def dot(a, b, dims=None):
    if dims is None:
        return jnp.dot(a, b, preferred_element_type=F32)
    return lax.dot_general(a, b, dims, preferred_element_type=F32)


VMEM = pl.BlockSpec(memory_space=pltpu.VMEM)
SMEM = pl.BlockSpec(memory_space=pltpu.SMEM)
ANY = pl.BlockSpec(memory_space=pltpu.HBM)


def call(body, operands, n_smem, outs, scratch=(), limit=8, flops=0, n_exp=0, n_any=0):
    shapes = [jax.ShapeDtypeStruct(s, t) for s, t in outs]
    cost = None
    if flops:
        cost = pl.CostEstimate(flops=flops, transcendentals=n_exp, bytes_accessed=4 * MIB)
    return pl.pallas_call(
        body,
        in_specs=[ANY] * n_any + [SMEM] * n_smem + [VMEM] * (len(operands) - n_smem - n_any),
        out_specs=[VMEM] * len(shapes),
        out_shape=shapes,
        scratch_shapes=list(scratch),
        cost_estimate=cost,
        compiler_params=pltpu.CompilerParams(vmem_limit_bytes=limit * MIB),
    )(*operands)


def gather_rows(pieces, gu, down):
    k = 0
    rows = down.shape[0]
    for ref in pieces:
        n, _, width, _ = ref.shape
        for i in range(n):
            gu[k * width : (k + 1) * width] = ref[i, 0]
            gu[rows + k * width : rows + (k + 1) * width] = ref[i, 1]
            down[k * width : (k + 1) * width] = ref[i, 2]
            k += 1


def mask_row(count, start, size, tokens):
    base = lax.axis_index("tok") * tokens + start
    return base + lax.broadcasted_iota(jnp.int32, (1, size), 1) < count


def inner_row(count, scale, rate, start, tokens):
    size = rate.shape[1]
    return jnp.where(mask_row(count, start, size, tokens), rate * -(scale / count.astype(F32)), 0.0)


def outer_row(count, start, size, tokens):
    return jnp.where(mask_row(count, start, size, tokens), 1.0, 0.0)


def tile_grads(x, e, row, gu, down):
    rows = down.shape[0]
    ab = dot(gu[...], x, NT)
    a = ab[:rows]
    b = ab[rows:]
    r = dot(down[...], e, NT) * row
    s = 0.5 + 0.5 * jnp.tanh(0.5 * a)
    act = a * s
    hidden = (act * b * row).astype(BF)
    e_up = (r * act).astype(BF)
    e_gate = (r * b * (s + act * (1.0 - s))).astype(BF)
    return ((e_gate, x), (e_up, x), (hidden, e))


def add_grads(pairs, i, steps, acc, out_ref, start=None):
    for j, (left, right) in enumerate(pairs):
        value = dot(left, right)
        if i > 0:
            value = value + acc[j]
        elif start is not None:
            value = value + start(j)
        if i == steps - 1:
            out_ref[j] = value.astype(out_ref.dtype)
        else:
            acc[j] = value


def grad_scratch(n_rows, dim):
    return [pltpu.VMEM((2 * n_rows, dim), BF), pltpu.VMEM((n_rows, dim), BF), pltpu.VMEM((3, n_rows, dim), F32)]


def grad_cost(tokens, n_rows, dim):
    return dict(limit=20, flops=12 * tokens * n_rows * dim, n_exp=tokens * n_rows)


def lead_body(keys_ref, values_ref, rate_hbm, gate_hbm, up_hbm, down_hbm, count_hbm, scale_ref, *refs):
    out_ref, x_ref, e_ref, first_ref, second_ref = refs[:5]
    gate_ref, up_ref, down_ref, gate_t, up_t, rate_ref, count_ref, gu, down, acc, sems = refs[5:]
    tokens = x_ref.shape[0]
    steps = tokens // TILE
    spans = [slice(i * TILE, (i + 1) * TILE) for i in range(steps)]
    copies = [(gate_hbm, gate_ref), (up_hbm, up_ref), (down_hbm, down_ref)]
    copies += [(count_hbm, count_ref), (rate_hbm, rate_ref)]
    for span in spans:
        copies += [(keys_ref.at[0, 0, span], x_ref.at[span]), (values_ref.at[0, 0, span], e_ref.at[span])]
    copies = [pltpu.make_async_copy(a, b, sems.at[n]) for n, (a, b) in enumerate(copies)]
    for copy in copies:
        copy.start()
    where = lax.axis_index("tok")
    z = where // 2
    core = where % 2
    chips, _, width, _ = first_ref.shape
    copies[0].wait()
    gate_t[...] = gate_ref[...].T
    copies[1].wait()
    up_t[...] = up_ref[...].T
    copies[2].wait()
    for half, out in enumerate((first_ref, second_ref)):
        for k in range(chips):
            owner = 2 * ((z + k) % chips) + (core + half) % 2
            rows = pl.ds(pl.multiple_of(owner * width, width), width)
            out[k, 0] = gate_t[rows, :]
            out[k, 1] = up_t[rows, :]
            out[k, 2] = down_ref[rows, :]
    gather_rows((second_ref,), gu, down)
    for n in range(3, 5):
        copies[n].wait()
    for i, span in enumerate(spans):
        copies[5 + 2 * i].wait()
        copies[6 + 2 * i].wait()
        row = inner_row(count_ref[0, 0], scale_ref[0], rate_ref[0, 0:1, span], i * TILE, tokens)
        pairs = tile_grads(x_ref[span], e_ref[span], row, gu, down)
        add_grads(pairs, i, steps, acc, out_ref)


def lead(keys, values, rate, w_gate, w_up, w_down, count, scale, parts):
    tokens, dim = keys.shape[2:]
    hid = w_gate.shape[1]
    half = hid // 2
    piece = (parts // 2, 3, hid // parts, dim)
    outs = [((3, half, dim), BF), ((tokens, dim), BF), ((tokens, dim), BF), (piece, BF), (piece, BF)]
    scratch = [pltpu.VMEM(w.shape, BF) for w in (w_gate, w_up, w_down)]
    scratch += [pltpu.VMEM((hid, dim), BF)] * 2
    scratch += [pltpu.VMEM(rate.shape, F32), pltpu.SMEM(count.shape, jnp.int32)]
    scratch += grad_scratch(half, dim) + [pltpu.SemaphoreType.DMA((5 + 2 * (tokens // TILE),))]
    operands = (keys, values, rate, w_gate, w_up, w_down, count)
    operands = [pltpu.with_memory_space_constraint(array, pltpu.HBM) for array in operands] + [scale]
    return call(lead_body, operands, 1, outs, scratch, n_any=7, **grad_cost(tokens, half, dim))


def grads_body(inner, block, n_pieces, skip, result, count_ref, scale_ref, rate_ref, x_ref, e_ref, *refs):
    pieces = refs[:n_pieces]
    refs = refs[n_pieces:]
    start = None
    if skip is not None:
        start_ref = refs[0]
        refs = refs[1:]
    out_ref, gu, down, acc = refs[0], *refs[-3:]
    gather_rows(pieces, gu, down)
    rows = down.shape[0]
    if skip is not None:
        start = lambda j: start_ref[j, skip : skip + rows]
    flat = len(x_ref.shape) == 2
    tokens = x_ref.shape[-2]
    count = count_ref[0, block]
    steps = tokens // TILE
    for i in range(steps):
        span = slice(i * TILE, (i + 1) * TILE)
        x = x_ref[span] if flat else x_ref[0, block, span]
        e = e_ref[span] if flat else e_ref[0, block, span]
        if inner:
            row = inner_row(count, scale_ref[0], rate_ref[0, block : block + 1, span], i * TILE, tokens)
        else:
            row = outer_row(count, i * TILE, TILE, tokens)
        pairs = tile_grads(x, e, row, gu, down)
        add_grads(pairs, i, steps, acc, out_ref, start)
        if result:
            refs[1][span] = dot(pairs[2][0], down[...], TN).astype(BF)


def grads(inner, block, args, x, e, pieces, out_dtype, acc=None, skip=None, result=False):
    tokens, dim = x.shape[-2:]
    n_rows = sum(p.shape[0] * p.shape[2] for p in pieces)
    operands = [*args, x, e, *pieces]
    if acc is not None:
        operands.append(acc)
    outs = [((3, n_rows, dim), out_dtype)]
    if result:
        outs.append(((tokens, dim), BF))
    return call(
        functools.partial(grads_body, inner, block, len(pieces), skip, result),
        operands,
        2,
        outs,
        grad_scratch(n_rows, dim),
        **grad_cost(tokens, n_rows, dim),
    )


def output_body(block, n_pieces, count_ref, x_ref, done_ref, *refs):
    out_ref, gu, down = refs[-3:]
    gather_rows(refs[:n_pieces], gu, down)
    rows = down.shape[0]
    tokens = x_ref.shape[2]
    for other in range(block):
        out_ref[0, other] = done_ref[...]
    for i in range(tokens // TILE):
        span = slice(i * TILE, (i + 1) * TILE)
        valid = mask_row(count_ref[0, block], i * TILE, TILE, tokens)
        ab = dot(gu[...], x_ref[0, block, span], NT)
        a = ab[:rows]
        s = 0.5 + 0.5 * jnp.tanh(0.5 * a)
        hidden = jnp.where(valid, a * s * ab[rows:], 0.0).astype(BF)
        out_ref[0, block, span] = dot(hidden, down[...], TN).astype(BF)


def output_of(count, x, done, pieces):
    tokens, dim = x.shape[2:]
    n_rows = sum(p.shape[0] * p.shape[2] for p in pieces)
    return call(
        functools.partial(output_body, 1, len(pieces)),
        [count, x, done, *pieces],
        1,
        [(x.shape, BF)],
        scratch=[pltpu.VMEM((2 * n_rows, dim), BF), pltpu.VMEM((n_rows, dim), BF)],
        limit=16,
        flops=6 * tokens * n_rows * dim,
        n_exp=tokens * n_rows,
    )[0]


def combine_body(own_ref, other_ref, *outs):
    width = outs[0].shape[1]
    for k, out in enumerate(outs):
        rows = slice(k * width, (k + 1) * width)
        out[...] = (own_ref[:, rows, :].astype(F32) + other_ref[:, rows, :].astype(F32)).astype(out.dtype)


def combine(own, other, chips):
    shape = (3, own.shape[1] // chips, own.shape[2])
    outs = [(shape, F32 if k == 0 else BF) for k in range(chips)]
    return call(combine_body, (own, other), 0, outs)


def norm_of(w):
    return jnp.sqrt(jnp.sum(w * w, axis=1, keepdims=True) + TINY)


def update_body(first, n_recv, scale_ref, own_ref, *refs):
    recv = refs[:n_recv]
    refs = refs[n_recv:]
    if first:
        start_ref, piece_ref, level_ref, state_out, momentum_out, norm_out = refs
    else:
        state_ref, momentum_ref, norm_ref, piece_ref, level_ref = refs
    scale = scale_ref[0]
    for j in range(3):
        total = own_ref[j]
        for ref in recv:
            total = total + ref[j].astype(F32)
        if j == 0:
            level = jnp.max(jnp.abs(total), axis=1, keepdims=True)
            level = jnp.broadcast_to(level, (level.shape[0], 128)).T
            level_ref[...] = level[: level_ref.shape[0]]
        if first:
            state = start_ref[0, j].astype(F32)
            norm = norm_of(state)
            moved = total / scale
        else:
            state = state_ref[j]
            norm = norm_ref[j][:, :1]
            moved = KEEP * momentum_ref[j] + total / scale
        state = state - RATE * moved
        state = state * (norm / norm_of(state))
        piece_ref[0, j] = state.astype(BF)
        if first:
            state_out[j] = state
            momentum_out[j] = moved
            norm_out[j] = jnp.broadcast_to(norm, norm_out.shape[1:])


def update(scale, own, recv, start=None, carried=None):
    first = start is not None
    operands = [scale, own, *recv] + ([start] if first else list(carried))
    outs = [((1,) + own.shape, BF), ((8, own.shape[1]), F32)]
    if first:
        outs += [(own.shape, F32), (own.shape, F32), (own.shape[:2] + (128,), F32)]
    return call(functools.partial(update_body, first, len(recv)), operands, 1, outs)


def write_payload(out_ref, totals, level):
    width = totals[0].shape[0]
    for j, total in enumerate(totals):
        out_ref[j * width : (j + 1) * width] = total.astype(BF)
    high = level.astype(BF).astype(F32)
    mid = (level - high).astype(BF).astype(F32)
    low = level - high - mid
    line = lax.broadcasted_iota(jnp.int32, level.shape, 0)
    terms = jnp.where(line == 0, high, jnp.where(line == 1, mid, jnp.where(line == 2, low, 0.0)))
    out_ref[len(totals) * width :] = terms.astype(BF)


def read_level(ref):
    terms = ref[ref.shape[0] - 8 :].astype(F32)
    return terms[0:1] + terms[1:2] + terms[2:3]


def pack_body(own_ref, one_ref, two_ref, three_ref, first_ref, second_ref, out_ref):
    totals = []
    for j in range(own_ref.shape[0]):
        total = own_ref[j]
        for ref in (one_ref, two_ref, three_ref):
            total = total + ref[j].astype(F32)
        totals.append(total)
    width = first_ref.shape[1]
    dim = own_ref.shape[2]
    gap = jnp.zeros((8, 128 - width), F32)
    rest = jnp.zeros((8, dim - 256), F32)
    level = jnp.concatenate([first_ref[...], gap, second_ref[...], gap, rest], axis=1)
    write_payload(out_ref, totals, level)


def pack(own, recv, first, second):
    n, width, dim = own.shape
    return call(pack_body, (own, *recv, first, second), 0, [((n * width + 8, dim), BF)])[0]


def sum_of(own_ref, recv, rows):
    one, two, three = [ref[rows].astype(F32) for ref in recv]
    return (own_ref[rows].astype(F32) + two) + (one + three)


def max_level(own_ref, recv):
    level = read_level(own_ref)
    for ref in recv:
        level = jnp.maximum(level, read_level(ref))
    return level


def mix_body(own_ref, one_ref, two_ref, three_ref, out_ref):
    recv = (one_ref, two_ref, three_ref)
    width = (own_ref.shape[0] - 8) // 3
    totals = [sum_of(own_ref, recv, slice(j * width, (j + 1) * width)) for j in range(3)]
    level = max_level(own_ref, recv)
    write_payload(out_ref, totals, jnp.broadcast_to(level, (8, level.shape[1])))


def mix(own, recv):
    return call(mix_body, (own, *recv), 0, [(own.shape, BF)])[0]


def finish_body(own_ref, one_ref, two_ref, three_ref, gate_ref, up_ref, down_ref, level_ref):
    recv = (one_ref, two_ref, three_ref)
    width = gate_ref.shape[0]
    for j, out in enumerate((gate_ref, up_ref, down_ref)):
        out[...] = sum_of(own_ref, recv, slice(j * width, (j + 1) * width))
    level = max_level(own_ref, recv)
    level_ref[0:1, :] = level[:, :width]
    level_ref[1:2, :] = level[:, 128 : 128 + width]


def finish(own, recv):
    rows, dim = own.shape
    width = (rows - 8) // 3
    outs = [((width, dim), F32)] * 3 + [((2, width), F32)]
    return call(finish_body, (own, *recv), 0, outs)


def per_device(
    keys, values, queries, token_rate, valid_count, loss_scale, w_gate, w_up, w_down, out_cotangent
):
    parts = lax.axis_size("tok")
    seqs = lax.axis_size("seq")
    chips = parts // 2
    side = math.isqrt(seqs)

    def z_shift(array, k):
        pairs = [(2 * z + c, 2 * ((z + k) % chips) + c) for z in range(chips) for c in range(2)]
        return lax.ppermute(array, "tok", pairs)

    def other_core(array):
        return lax.ppermute(array, "tok", [(t, t ^ 1) for t in range(parts)])

    def across(array, first):
        recv = []
        for k in range(1, side):
            pairs = []
            for t in range(parts):
                for y in range(side):
                    for x in range(side):
                        to = (y, (x + k) % side) if (t % 2 == 0) == first else ((y + k) % side, x)
                        pairs.append(((t * side + y) * side + x, (t * side + to[0]) * side + to[1]))
            recv.append(lax.ppermute(array, ("tok", "seq"), pairs))
        return recv

    def scatter(own, other):
        sums = combine(own, other_core(other), chips)
        recv = []
        for k in range(1, chips):
            recv.append(z_shift(sums[k], k))
        return sums[0], recv

    def spread(piece):
        mine = [piece] + [z_shift(piece, chips - k) for k in range(1, chips)]
        return mine, [other_core(p) for p in mine]

    half = w_gate.shape[1] // 2
    args = (valid_count, loss_scale, token_rate)
    other, x, e, first, _ = lead(
        keys, values, token_rate, w_gate, w_up, w_down, valid_count, loss_scale, parts
    )
    own = grads(True, 0, args, x, e, [first], F32)[0]
    own, recv = scatter(own, other)
    piece, level0, *carried = update(loss_scale, own, recv, start=first)
    halves = spread(piece)
    acc, done = grads(False, 0, args, queries, out_cotangent, halves[0] + halves[1], F32, result=True)
    other = grads(True, 1, args, keys, values, halves[1], BF)[0]
    own = grads(True, 1, args, keys, values, halves[0], F32)[0]
    own, recv = scatter(own, other)
    piece, level1 = update(loss_scale, own, recv, carried=carried)
    halves = spread(piece)
    other = grads(False, 1, args, queries, out_cotangent, halves[1], BF, acc=acc, skip=half)[0]
    own = grads(False, 1, args, queries, out_cotangent, halves[0], F32, acc=acc, skip=0)[0]
    own, recv = scatter(own, other)
    fast_out = output_of(valid_count, queries, done, halves[0] + halves[1])
    packed = pack(own, recv, level0, level1)
    packed = mix(packed, across(packed, True))
    gate, up, down, level = finish(packed, across(packed, False))
    return (fast_out, gate.T, up.T, down, level)


def solution(mesh):
    placed = (
        P("seq", None, "tok", None),
        P("seq", None, "tok", None),
        P("seq", None, "tok", None),
        P("seq", None, "tok"),
        P("seq", None),
        P(),
        P(),
        P(),
        P(),
        P("seq", None, "tok", None),
    )

    return jax.shard_map(
        per_device,
        mesh=mesh,
        in_specs=placed,
        out_specs=(
            P("seq", None, "tok", None),
            P(None, "tok"),
            P(None, "tok"),
            P("tok", None),
            P(None, "tok"),
        ),
        check_vma=False,
    )
```

time: 134 us -> 123 us (0.918)
  the two profiles are of different devices: /device:TPU:1 before, /device:TPU:0 now
where the time goes in v3:
time: 123 us; the launch traced here: 122 us
  waiting for transfers between devices  56.9 us (46%)
  starting transfers between devices  34.5 us (28%)
  Pallas kernels  29.6 us (24%)
  between operations  1.52 us (1%)
    ppermute x15, waiting for transfers between devices, z_shift(): return lax.ppermute(array, 'tok', pairs)  44 us
    pallas_call x16, Pallas kernels, call(): pl.pallas_call(body, in_specs=[ANY] * n_any + [SMEM] * n_smem + [VMEM] *...  29.6 us
    ppermute x15, starting transfers between devices, z_shift(): return lax.ppermute(array, 'tok', pairs)  23.8 us
    ppermute x6, waiting for transfers between devices, across(): recv.append(lax.ppermute(array, ('tok', 'seq'), pairs))  11.6 us
    ppermute x6, starting transfers between devices, across(): recv.append(lax.ppermute(array, ('tok', 'seq'), pairs))  9.17 us
  transfers between devices with their start and end apart: 32, of which 19 were waited for; matrix products, arithmetic and copies ran while one was open for 0% of the time, Pallas kernels for 14%

profile of v3, /device:TPU:0, one launch (start us, length us, event | category | flops | bytes accessed | tf_op | source)
XLA Modules:
  0.0 122.5 jit_solution(866137183005010240)
XLA Ops:
  1.3 4.7 %shard_map.137 = (bf16[3,256,512]{2,1,0:T(8,128)(2,1)S(1)}, bf16[1024,512]{1,0:T(8,128)(2,1)S(1)}, bf16[1024,512]{1,0:T(8,128)(2,1)S(1)}, bf16[4,3,64,512]{3,2,1,0:T(8,128)(2,1)S(1)}, bf16[4,3,64,512]{3,2,1,0:T(8,128)(2,1)}) custom-call(bf16[1,2,1024,512]{3,2,1,0:T(8,128)(2,1)} %x_ref.8, bf16[1,2,1024,512]{3,2,1,0:T(8,128)(2,1)} %e_ref.7, ...), custom_call_target="tpu_custom_call" | custom-call | flops 1610612736 | bytes 4194304 | tf_op jit(solution)/shard_map/pallas_call | solution.py:38
  6.2 2.6 %shard_map.138.own_ref = f32[3,256,512]{2,1,0:T(8,128)S(1)} custom-call(s32[1,2]{1,0:T(1,128)S(1)} %copy-done.5, f32[1]{0:T(128)S(6)} %copy.15.scale_ref, f32[1,2,1024]{2,1,0:T(2,128)S(1)} %copy-done.4, bf16[1024,512]{1,0:T(8,128)(2,1)S(1)} %get-tuple-element.34.x_ref, bf16[1024,512]{1,0:T(8,128)(2,1)S(1)} %get-tuple-element.35.e_ref, ...), custom_call_target="tpu_custom_call" | custom-call | flops 1610612736 | bytes 4194304 | tf_op jit(solution)/shard_map/pallas_call | solution.py:38
  9.0 2.1 %collective-permute-start.1 = (bf16[3,64,512]{2,1,0:T(8,128)(2,1)S(1)}, bf16[3,64,512]{2,1,0:T(8,128)(2,1)S(1)}, u32[]{:S(2)}, u32[]{:S(2)}) collective-permute-start(bf16[3,64,512]{2,1,0:T(8,128)(2,1)S(1)} %get-tuple-element.39), channel_id=1, source_target_pairs={{0,32},{16,48},{32,64},{48,80},{64,96},{80,112},{96,0},{112,16},{1... | collective-permute-start | bytes 589832 | tf_op jit(solution)/shard_map/ppermute | solution.py:393
  11.1 3.6 %collective-permute-start.2 = (bf16[3,64,512]{2,1,0:T(8,128)(2,1)S(1)}, bf16[3,64,512]{2,1,0:T(8,128)(2,1)S(1)}, u32[]{:S(2)}, u32[]{:S(2)}) collective-permute-start(bf16[3,64,512]{2,1,0:T(8,128)(2,1)S(1)} %get-tuple-element.40), channel_id=1, source_target_pairs={{0,64},{16,80},{32,96},{48,112},{64,0},{80,16},{96,32},{112,48},{1... | collective-permute-start | bytes 589832 | tf_op jit(solution)/shard_map/ppermute | solution.py:393
  15.7 3.1 %collective-permute-done.1.refs_0_ = bf16[3,64,512]{2,1,0:T(8,128)(2,1)S(1)} collective-permute-done((bf16[3,64,512]{2,1,0:T(8,128)(2,1)S(1)}, bf16[3,64,512]{2,1,0:T(8,128)(2,1)S(1)}, u32[]{:S(2)}, u32[]{:S(2)}) %collective-permute-start.1) | collective-permute-done | bytes 196640 | tf_op jit(solution)/shard_map/ppermute | solution.py:393
  18.8 5.4 %collective-permute-done.2.refs_1_ = bf16[3,64,512]{2,1,0:T(8,128)(2,1)S(1)} collective-permute-done((bf16[3,64,512]{2,1,0:T(8,128)(2,1)S(1)}, bf16[3,64,512]{2,1,0:T(8,128)(2,1)S(1)}, u32[]{:S(2)}, u32[]{:S(2)}) %collective-permute-start.2) | collective-permute-done | bytes 196640 | tf_op jit(solution)/shard_map/ppermute | solution.py:393
  24.4 1.3 %collective-permute-start.6 = (bf16[1,3,64,512]{3,2,1,0:T(8,128)(2,1)S(1)}, bf16[1,3,64,512]{3,2,1,0:T(8,128)(2,1)S(1)}, u32[]{:S(2)}, u32[]{:S(2)}) collective-permute-start(bf16[1,3,64,512]{3,2,1,0:T(8,128)(2,1)S(1)} %get-tuple-element.42.refs_0_), channel_id=1, source_target_pairs={{0,32},{16,48},{32,64},{48,80},{64,96},{80,112},{96,0},{112,16},{1... | collective-permute-start | bytes 589832 | tf_op jit(solution)/shard_map/ppermute | solution.py:393
  25.7 2.4 %collective-permute-start.5 = (bf16[1,3,64,512]{3,2,1,0:T(8,128)(2,1)S(1)}, bf16[1,3,64,512]{3,2,1,0:T(8,128)(2,1)S(1)}, u32[]{:S(2)}, u32[]{:S(2)}) collective-permute-start(bf16[1,3,64,512]{3,2,1,0:T(8,128)(2,1)S(1)} %get-tuple-element.42.refs_0_), channel_id=1, source_target_pairs={{0,64},{16,80},{32,96},{48,112},{64,0},{80,16},{96,32},{112,48},{1... | collective-permute-start | bytes 589832 | tf_op jit(solution)/shard_map/ppermute | solution.py:393
  29.4 2.9 %collective-permute-done.6.refs_3_ = bf16[1,3,64,512]{3,2,1,0:T(8,128)(2,1)S(1)} collective-permute-done((bf16[1,3,64,512]{3,2,1,0:T(8,128)(2,1)S(1)}, bf16[1,3,64,512]{3,2,1,0:T(8,128)(2,1)S(1)}, u32[]{:S(2)}, u32[]{:S(2)}) %collective-permute-start.6) | collective-permute-done | bytes 196640 | tf_op jit(solution)/shard_map/ppermute | solution.py:393
  32.3 4.8 %collective-permute-done.5.refs_2_ = bf16[1,3,64,512]{3,2,1,0:T(8,128)(2,1)S(1)} collective-permute-done((bf16[1,3,64,512]{3,2,1,0:T(8,128)(2,1)S(1)}, bf16[1,3,64,512]{3,2,1,0:T(8,128)(2,1)S(1)}, u32[]{:S(2)}, u32[]{:S(2)}) %collective-permute-start.5) | collective-permute-done | bytes 196640 | tf_op jit(solution)/shard_map/ppermute | solution.py:393
  38.9 2.7 %shard_map.143 = bf16[3,256,512]{2,1,0:T(8,128)(2,1)S(1)} custom-call(s32[1,2]{1,0:T(1,128)S(1)} %copy-done.5, f32[1]{0:T(128)S(6)} %copy.15.scale_ref, f32[1,2,1024]{2,1,0:T(2,128)S(1)} %copy-done.4, bf16[1,2,1024,512]{3,2,1,0:T(8,128)(2,1)S(1)} %copy-done.2, bf16[1,2,1024,512]{3,2,1,0:T(8,128)(2,1)S(1)} %copy-done.3, ...), custom_call_target="tpu_custom_call" | custom-call | flops 1610612736 | bytes 4194304 | tf_op jit(solution)/shard_map/pallas_call | solution.py:38
  41.9 2.7 %shard_map.142.own_ref = f32[3,256,512]{2,1,0:T(8,128)S(1)} custom-call(s32[1,2]{1,0:T(1,128)S(1)} %copy-done.5, f32[1]{0:T(128)S(6)} %copy.15.scale_ref, f32[1,2,1024]{2,1,0:T(2,128)S(1)} %copy-done.4, bf16[1,2,1024,512]{3,2,1,0:T(8,128)(2,1)S(1)} %copy-done.2, bf16[1,2,1024,512]{3,2,1,0:T(8,128)(2,1)S(1)} %copy-done.3, ...), custom_call_target="tpu_custom_call" | custom-call | flops 1610612736 | bytes 4194304 | tf_op jit(solution)/shard_map/pallas_call | solution.py:38
  45.9 2.8 %collective-permute-start.13 = (bf16[3,64,512]{2,1,0:T(8,128)(2,1)S(1)}, bf16[3,64,512]{2,1,0:T(8,128)(2,1)S(1)}, u32[]{:S(2)}, u32[]{:S(2)}) collective-permute-start(bf16[3,64,512]{2,1,0:T(8,128)(2,1)S(1)} %get-tuple-element.46), channel_id=1, source_target_pairs={{0,64},{16,80},{32,96},{48,112},{64,0},{80,16},{96,32},{112,48},{1... | collective-permute-start | bytes 589832 | tf_op jit(solution)/shard_map/ppermute | solution.py:393
  49.1 4.4 %collective-permute-done.12.refs_0_ = bf16[3,64,512]{2,1,0:T(8,128)(2,1)S(1)} collective-permute-done((bf16[3,64,512]{2,1,0:T(8,128)(2,1)S(1)}, bf16[3,64,512]{2,1,0:T(8,128)(2,1)S(1)}, u32[]{:S(2)}, u32[]{:S(2)}) %collective-permute-start.12) | collective-permute-done | bytes 196640 | tf_op jit(solution)/shard_map/ppermute | solution.py:393
  53.6 4.4 %collective-permute-done.13.refs_1_ = bf16[3,64,512]{2,1,0:T(8,128)(2,1)S(1)} collective-permute-done((bf16[3,64,512]{2,1,0:T(8,128)(2,1)S(1)}, bf16[3,64,512]{2,1,0:T(8,128)(2,1)S(1)}, u32[]{:S(2)}, u32[]{:S(2)}) %collective-permute-start.13) | collective-permute-done | bytes 196640 | tf_op jit(solution)/shard_map/ppermute | solution.py:393
  59.5 3.3 %collective-permute-start.16 = (bf16[1,3,64,512]{3,2,1,0:T(8,128)(2,1)S(1)}, bf16[1,3,64,512]{3,2,1,0:T(8,128)(2,1)S(1)}, u32[]{:S(2)}, u32[]{:S(2)}) collective-permute-start(bf16[1,3,64,512]{3,2,1,0:T(8,128)(2,1)S(1)} %get-tuple-element.51.refs_0_), channel_id=1, source_target_pairs={{0,64},{16,80},{32,96},{48,112},{64,0},{80,16},{96,32},{112,48},{1... | collective-permute-start | bytes 589832 | tf_op jit(solution)/shard_map/ppermute | solution.py:393
  62.8 3.6 %collective-permute-done.17.refs_3_ = bf16[1,3,64,512]{3,2,1,0:T(8,128)(2,1)S(1)} collective-permute-done((bf16[1,3,64,512]{3,2,1,0:T(8,128)(2,1)S(1)}, bf16[1,3,64,512]{3,2,1,0:T(8,128)(2,1)S(1)}, u32[]{:S(2)}, u32[]{:S(2)}) %collective-permute-start.17) | collective-permute-done | bytes 196640 | tf_op jit(solution)/shard_map/ppermute | solution.py:393
  66.4 5.4 %collective-permute-done.16.refs_2_ = bf16[1,3,64,512]{3,2,1,0:T(8,128)(2,1)S(1)} collective-permute-done((bf16[1,3,64,512]{3,2,1,0:T(8,128)(2,1)S(1)}, bf16[1,3,64,512]{3,2,1,0:T(8,128)(2,1)S(1)}, u32[]{:S(2)}, u32[]{:S(2)}) %collective-permute-start.16) | collective-permute-done | bytes 196640 | tf_op jit(solution)/shard_map/ppermute | solution.py:393
  72.3 5.1 %shard_map.141 = (f32[3,512,512]{2,1,0:T(8,128)S(1)}, bf16[1024,512]{1,0:T(8,128)(2,1)S(1)}) custom-call(s32[1,2]{1,0:T(1,128)S(1)} %copy-done.5, f32[1]{0:T(128)S(6)} %copy.15.scale_ref, f32[1,2,1024]{2,1,0:T(2,128)S(1)} %copy-done.4, bf16[1,2,1024,512]{3,2,1,0:T(8,128)(2,1)S(1)} %copy-done, bf16[1,2,1024,512]{3,2,1,0:T(8,128)(2,1)S(1)} %copy-done.1, ...), custom_call_target="tpu_custom_call" | custom-call | flops 3221225472 | bytes 4194304 | tf_op jit(solution)/shard_map/pallas_call | solution.py:38
  77.5 2.7 %shard_map.148 = bf16[3,256,512]{2,1,0:T(8,128)(2,1)S(1)} custom-call(s32[1,2]{1,0:T(1,128)S(1)} %copy-done.5, f32[1]{0:T(128)S(6)} %copy.15.scale_ref, f32[1,2,1024]{2,1,0:T(2,128)S(1)} %copy-done.4, bf16[1,2,1024,512]{3,2,1,0:T(8,128)(2,1)S(1)} %copy-done, bf16[1,2,1024,512]{3,2,1,0:T(8,128)(2,1)S(1)} %copy-done.1, ...), custom_call_target="tpu_custom_call" | custom-call | flops 1610612736 | bytes 4194304 | tf_op jit(solution)/shard_map/pallas_call | solution.py:38
  80.3 2.7 %shard_map.147.own_ref = f32[3,256,512]{2,1,0:T(8,128)S(1)} custom-call(s32[1,2]{1,0:T(1,128)S(1)} %copy-done.5, f32[1]{0:T(128)S(6)} %copy.15.scale_ref, f32[1,2,1024]{2,1,0:T(2,128)S(1)} %copy-done.4, bf16[1,2,1024,512]{3,2,1,0:T(8,128)(2,1)S(1)} %copy-done, bf16[1,2,1024,512]{3,2,1,0:T(8,128)(2,1)S(1)} %copy-done.1, ...), custom_call_target="tpu_custom_call" | custom-call | flops 1610612736 | bytes 4194304 | tf_op jit(solution)/shard_map/pallas_call | solution.py:38
  83.7 3.3 %collective-permute-start.24 = (bf16[3,64,512]{2,1,0:T(8,128)(2,1)S(1)}, bf16[3,64,512]{2,1,0:T(8,128)(2,1)S(1)}, u32[]{:S(2)}, u32[]{:S(2)}) collective-permute-start(bf16[3,64,512]{2,1,0:T(8,128)(2,1)S(1)} %get-tuple-element.55), channel_id=1, source_target_pairs={{0,64},{16,80},{32,96},{48,112},{64,0},{80,16},{96,32},{112,48},{1... | collective-permute-start | bytes 589832 | tf_op jit(solution)/shard_map/ppermute | solution.py:393
  87.0 5.8 %collective-permute-done.23.one_ref = bf16[3,64,512]{2,1,0:T(8,128)(2,1)S(1)} collective-permute-done((bf16[3,64,512]{2,1,0:T(8,128)(2,1)S(1)}, bf16[3,64,512]{2,1,0:T(8,128)(2,1)S(1)}, u32[]{:S(2)}, u32[]{:S(2)}) %collective-permute-start.23) | collective-permute-done | bytes 196640 | tf_op jit(solution)/shard_map/ppermute | solution.py:393
  92.8 3.3 %collective-permute-done.24.two_ref = bf16[3,64,512]{2,1,0:T(8,128)(2,1)S(1)} collective-permute-done((bf16[3,64,512]{2,1,0:T(8,128)(2,1)S(1)}, bf16[3,64,512]{2,1,0:T(8,128)(2,1)S(1)}, u32[]{:S(2)}, u32[]{:S(2)}) %collective-permute-start.24) | collective-permute-done | bytes 196640 | tf_op jit(solution)/shard_map/ppermute | solution.py:393
  96.8 2.8 %collective-permute-start.28 = (bf16[200,512]{1,0:T(8,128)(2,1)S(1)}, bf16[200,512]{1,0:T(8,128)(2,1)S(1)}, u32[]{:S(2)}, u32[]{:S(2)}) collective-permute-start(bf16[200,512]{1,0:T(8,128)(2,1)S(1)} %shard_map.150.own_ref), channel_id=1, source_target_pairs={{0,3},{1,0},{2,1},{3,2},{4,7},{5,4},{6,5},{7,6},{8,11},{9,8},{10,9... | collective-permute-start | bytes 614408 | tf_op jit(solution)/shard_map/ppermute | solution.py:407
  101.3 3.8 %collective-permute-done.28.three_ref = bf16[200,512]{1,0:T(8,128)(2,1)S(1)} collective-permute-done((bf16[200,512]{1,0:T(8,128)(2,1)S(1)}, bf16[200,512]{1,0:T(8,128)(2,1)S(1)}, u32[]{:S(2)}, u32[]{:S(2)}) %collective-permute-start.28) | collective-permute-done | bytes 204832 | tf_op jit(solution)/shard_map/ppermute | solution.py:407
  105.1 1.9 %collective-permute-done.27.two_ref = bf16[200,512]{1,0:T(8,128)(2,1)S(1)} collective-permute-done((bf16[200,512]{1,0:T(8,128)(2,1)S(1)}, bf16[200,512]{1,0:T(8,128)(2,1)S(1)}, u32[]{:S(2)}, u32[]{:S(2)}) %collective-permute-start.27) | collective-permute-done | bytes 204832 | tf_op jit(solution)/shard_map/ppermute | solution.py:407
  107.0 2.1 %collective-permute-done.26.one_ref = bf16[200,512]{1,0:T(8,128)(2,1)S(1)} collective-permute-done((bf16[200,512]{1,0:T(8,128)(2,1)S(1)}, bf16[200,512]{1,0:T(8,128)(2,1)S(1)}, u32[]{:S(2)}, u32[]{:S(2)}) %collective-permute-start.26) | collective-permute-done | bytes 204832 | tf_op jit(solution)/shard_map/ppermute | solution.py:407
  109.2 3.1 %collective-permute-start.31 = (bf16[200,512]{1,0:T(8,128)(2,1)S(1)}, bf16[200,512]{1,0:T(8,128)(2,1)S(1)}, u32[]{:S(2)}, u32[]{:S(2)}) collective-permute-start(bf16[200,512]{1,0:T(8,128)(2,1)S(1)} %shard_map.151.own_ref), channel_id=1, source_target_pairs={{0,12},{1,13},{2,14},{3,15},{4,0},{5,1},{6,2},{7,3},{8,4},{9,5},{1... | collective-permute-start | bytes 614408 | tf_op jit(solution)/shard_map/ppermute | solution.py:407
  113.9 4.0 %shard_map.146 = bf16[1,2,1024,512]{3,2,1,0:T(8,128)(2,1)} custom-call(s32[1,2]{1,0:T(1,128)S(1)} %copy-done.5, bf16[1,2,1024,512]{3,2,1,0:T(8,128)(2,1)S(1)} %copy-done, bf16[1024,512]{1,0:T(8,128)(2,1)S(1)} %get-tuple-element.43.done_ref, bf16[1,3,64,512]{3,2,1,0:T(8,128)(2,1)S(1)} %get-tuple-element.51.refs_0_, ...), custom_call_target="tpu_custom_call" | custom-call | flops 1610612736 | bytes 4194304 | tf_op jit(solution)/shard_map/pallas_call | solution.py:38
  117.8 1.8 %collective-permute-done.30.two_ref = bf16[200,512]{1,0:T(8,128)(2,1)S(1)} collective-permute-done((bf16[200,512]{1,0:T(8,128)(2,1)S(1)}, bf16[200,512]{1,0:T(8,128)(2,1)S(1)}, u32[]{:S(2)}, u32[]{:S(2)}) %collective-permute-start.30) | collective-permute-done | bytes 204832 | tf_op jit(solution)/shard_map/ppermute | solution.py:407
  119.6 2.1 %collective-permute-done.29.one_ref = bf16[200,512]{1,0:T(8,128)(2,1)S(1)} collective-permute-done((bf16[200,512]{1,0:T(8,128)(2,1)S(1)}, bf16[200,512]{1,0:T(8,128)(2,1)S(1)}, u32[]{:S(2)}, u32[]{:S(2)}) %collective-permute-start.29) | collective-permute-done | bytes 204832 | tf_op jit(solution)/shard_map/ppermute | solution.py:407
  (60 shorter events, 14.1 us)
Async XLA Ops:
  6.0 2.8 %collective-permute-start = (bf16[3,256,512]{2,1,0:T(8,128)(2,1)S(1)}, bf16[3,256,512]{2,1,0:T(8,128)(2,1)S(1)}, u32[]{:S(2)}, u32[]{:S(2)}) collective-permute-start(bf16[3,256,512]{2,1,0:T(8,128)(2,1)S(1)} %get-tuple-element.37), channel_id=1, source_target_pairs={{0,16},{16,0},{32,48},{48,32},{64,80},{80,64},{96,112},{112,96},{1... | collective-permute-start | bytes 2359304 | tf_op jit(solution)/shard_map/ppermute | solution.py:396
  9.0 9.8 %collective-permute-start.1 = (bf16[3,64,512]{2,1,0:T(8,128)(2,1)S(1)}, bf16[3,64,512]{2,1,0:T(8,128)(2,1)S(1)}, u32[]{:S(2)}, u32[]{:S(2)}) collective-permute-start(bf16[3,64,512]{2,1,0:T(8,128)(2,1)S(1)} %get-tuple-element.39), channel_id=1, source_target_pairs={{0,32},{16,48},{32,64},{48,80},{64,96},{80,112},{96,0},{112,16},{1... | collective-permute-start | bytes 589832 | tf_op jit(solution)/shard_map/ppermute | solution.py:393
  11.1 13.1 %collective-permute-start.2 = (bf16[3,64,512]{2,1,0:T(8,128)(2,1)S(1)}, bf16[3,64,512]{2,1,0:T(8,128)(2,1)S(1)}, u32[]{:S(2)}, u32[]{:S(2)}) collective-permute-start(bf16[3,64,512]{2,1,0:T(8,128)(2,1)S(1)} %get-tuple-element.40), channel_id=1, source_target_pairs={{0,64},{16,80},{32,96},{48,112},{64,0},{80,16},{96,32},{112,48},{1... | collective-permute-start | bytes 589832 | tf_op jit(solution)/shard_map/ppermute | solution.py:393
  14.7 9.5 %collective-permute-start.3 = (bf16[3,64,512]{2,1,0:T(8,128)(2,1)S(1)}, bf16[3,64,512]{2,1,0:T(8,128)(2,1)S(1)}, u32[]{:S(2)}, u32[]{:S(2)}) collective-permute-start(bf16[3,64,512]{2,1,0:T(8,128)(2,1)S(1)} %get-tuple-element.41), channel_id=1, source_target_pairs={{0,96},{16,112},{32,0},{48,16},{64,32},{80,48},{96,64},{112,80},{1... | collective-permute-start | bytes 589832 | tf_op jit(solution)/shard_map/ppermute | solution.py:393
  24.4 7.9 %collective-permute-start.6 = (bf16[1,3,64,512]{3,2,1,0:T(8,128)(2,1)S(1)}, bf16[1,3,64,512]{3,2,1,0:T(8,128)(2,1)S(1)}, u32[]{:S(2)}, u32[]{:S(2)}) collective-permute-start(bf16[1,3,64,512]{3,2,1,0:T(8,128)(2,1)S(1)} %get-tuple-element.42.refs_0_), channel_id=1, source_target_pairs={{0,32},{16,48},{32,64},{48,80},{64,96},{80,112},{96,0},{112,16},{1... | collective-permute-start | bytes 589832 | tf_op jit(solution)/shard_map/ppermute | solution.py:393
  25.7 11.4 %collective-permute-start.5 = (bf16[1,3,64,512]{3,2,1,0:T(8,128)(2,1)S(1)}, bf16[1,3,64,512]{3,2,1,0:T(8,128)(2,1)S(1)}, u32[]{:S(2)}, u32[]{:S(2)}) collective-permute-start(bf16[1,3,64,512]{3,2,1,0:T(8,128)(2,1)S(1)} %get-tuple-element.42.refs_0_), channel_id=1, source_target_pairs={{0,64},{16,80},{32,96},{48,112},{64,0},{80,16},{96,32},{112,48},{1... | collective-permute-start | bytes 589832 | tf_op jit(solution)/shard_map/ppermute | solution.py:393
  28.1 9.0 %collective-permute-start.4 = (bf16[1,3,64,512]{3,2,1,0:T(8,128)(2,1)S(1)}, bf16[1,3,64,512]{3,2,1,0:T(8,128)(2,1)S(1)}, u32[]{:S(2)}, u32[]{:S(2)}) collective-permute-start(bf16[1,3,64,512]{3,2,1,0:T(8,128)(2,1)S(1)} %get-tuple-element.42.refs_0_), channel_id=1, source_target_pairs={{0,96},{16,112},{32,0},{48,16},{64,32},{80,48},{96,64},{112,80},{1... | collective-permute-start | bytes 589832 | tf_op jit(solution)/shard_map/ppermute | solution.py:393
  29.4 8.3 %collective-permute-start.7 = (bf16[1,3,64,512]{3,2,1,0:T(8,128)(2,1)S(1)}, bf16[1,3,64,512]{3,2,1,0:T(8,128)(2,1)S(1)}, u32[]{:S(2)}, u32[]{:S(2)}) collective-permute-start(bf16[1,3,64,512]{3,2,1,0:T(8,128)(2,1)S(1)} %get-tuple-element.42.refs_0_), channel_id=1, source_target_pairs={{0,16},{16,0},{32,48},{48,32},{64,80},{80,64},{96,112},{112,96},{1... | collective-permute-start | bytes 589832 | tf_op jit(solution)/shard_map/ppermute | solution.py:396
  32.3 5.4 %collective-permute-start.10 = (bf16[1,3,64,512]{3,2,1,0:T(8,128)(2,1)S(1)}, bf16[1,3,64,512]{3,2,1,0:T(8,128)(2,1)S(1)}, u32[]{:S(2)}, u32[]{:S(2)}) collective-permute-start(bf16[1,3,64,512]{3,2,1,0:T(8,128)(2,1)S(1)} %collective-permute-done.6.refs_3_), channel_id=1, source_target_pairs={{0,16},{16,0},{32,48},{48,32},{64,80},{80,64},{96,112},{112,96},{1... | collective-permute-start | bytes 589832 | tf_op jit(solution)/shard_map/ppermute | solution.py:396
  37.1 1.4 %collective-permute-start.9 = (bf16[1,3,64,512]{3,2,1,0:T(8,128)(2,1)S(1)}, bf16[1,3,64,512]{3,2,1,0:T(8,128)(2,1)S(1)}, u32[]{:S(2)}, u32[]{:S(2)}) collective-permute-start(bf16[1,3,64,512]{3,2,1,0:T(8,128)(2,1)S(1)} %collective-permute-done.5.refs_2_), channel_id=1, source_target_pairs={{0,16},{16,0},{32,48},{48,32},{64,80},{80,64},{96,112},{112,96},{1... | collective-permute-start | bytes 589832 | tf_op jit(solution)/shard_map/ppermute | solution.py:396
  37.2 1.7 %collective-permute-start.8 = (bf16[1,3,64,512]{3,2,1,0:T(8,128)(2,1)S(1)}, bf16[1,3,64,512]{3,2,1,0:T(8,128)(2,1)S(1)}, u32[]{:S(2)}, u32[]{:S(2)}) collective-permute-start(bf16[1,3,64,512]{3,2,1,0:T(8,128)(2,1)S(1)} %collective-permute-done.4.refs_1_), channel_id=1, source_target_pairs={{0,16},{16,0},{32,48},{48,32},{64,80},{80,64},{96,112},{112,96},{1... | collective-permute-start | bytes 589832 | tf_op jit(solution)/shard_map/ppermute | solution.py:396
  41.6 3.1 %collective-permute-start.11 = (bf16[3,256,512]{2,1,0:T(8,128)(2,1)S(1)}, bf16[3,256,512]{2,1,0:T(8,128)(2,1)S(1)}, u32[]{:S(2)}, u32[]{:S(2)}) collective-permute-start(bf16[3,256,512]{2,1,0:T(8,128)(2,1)S(1)} %shard_map.143), channel_id=1, source_target_pairs={{0,16},{16,0},{32,48},{48,32},{64,80},{80,64},{96,112},{112,96},{1... | collective-permute-start | bytes 2359304 | tf_op jit(solution)/shard_map/ppermute | solution.py:396
  44.9 8.7 %collective-permute-start.12 = (bf16[3,64,512]{2,1,0:T(8,128)(2,1)S(1)}, bf16[3,64,512]{2,1,0:T(8,128)(2,1)S(1)}, u32[]{:S(2)}, u32[]{:S(2)}) collective-permute-start(bf16[3,64,512]{2,1,0:T(8,128)(2,1)S(1)} %get-tuple-element.45), channel_id=1, source_target_pairs={{0,32},{16,48},{32,64},{48,80},{64,96},{80,112},{96,0},{112,16},{1... | collective-permute-start | bytes 589832 | tf_op jit(solution)/shard_map/ppermute | solution.py:393
  45.9 12.2 %collective-permute-start.13 = (bf16[3,64,512]{2,1,0:T(8,128)(2,1)S(1)}, bf16[3,64,512]{2,1,0:T(8,128)(2,1)S(1)}, u32[]{:S(2)}, u32[]{:S(2)}) collective-permute-start(bf16[3,64,512]{2,1,0:T(8,128)(2,1)S(1)} %get-tuple-element.46), channel_id=1, source_target_pairs={{0,64},{16,80},{32,96},{48,112},{64,0},{80,16},{96,32},{112,48},{1... | collective-permute-start | bytes 589832 | tf_op jit(solution)/shard_map/ppermute | solution.py:393
  48.7 9.6 %collective-permute-start.14 = (bf16[3,64,512]{2,1,0:T(8,128)(2,1)S(1)}, bf16[3,64,512]{2,1,0:T(8,128)(2,1)S(1)}, u32[]{:S(2)}, u32[]{:S(2)}) collective-permute-start(bf16[3,64,512]{2,1,0:T(8,128)(2,1)S(1)} %get-tuple-element.47), channel_id=1, source_target_pairs={{0,96},{16,112},{32,0},{48,16},{64,32},{80,48},{96,64},{112,80},{1... | collective-permute-start | bytes 589832 | tf_op jit(solution)/shard_map/ppermute | solution.py:393
  58.6 7.8 %collective-permute-start.17 = (bf16[1,3,64,512]{3,2,1,0:T(8,128)(2,1)S(1)}, bf16[1,3,64,512]{3,2,1,0:T(8,128)(2,1)S(1)}, u32[]{:S(2)}, u32[]{:S(2)}) collective-permute-start(bf16[1,3,64,512]{3,2,1,0:T(8,128)(2,1)S(1)} %get-tuple-element.51.refs_0_), channel_id=1, source_target_pairs={{0,32},{16,48},{32,64},{48,80},{64,96},{80,112},{96,0},{112,16},{1... | collective-permute-start | bytes 589832 | tf_op jit(solution)/shard_map/ppermute | solution.py:393
  59.5 12.3 %collective-permute-start.16 = (bf16[1,3,64,512]{3,2,1,0:T(8,128)(2,1)S(1)}, bf16[1,3,64,512]{3,2,1,0:T(8,128)(2,1)S(1)}, u32[]{:S(2)}, u32[]{:S(2)}) collective-permute-start(bf16[1,3,64,512]{3,2,1,0:T(8,128)(2,1)S(1)} %get-tuple-element.51.refs_0_), channel_id=1, source_target_pairs={{0,64},{16,80},{32,96},{48,112},{64,0},{80,16},{96,32},{112,48},{1... | collective-permute-start | bytes 589832 | tf_op jit(solution)/shard_map/ppermute | solution.py:393
  62.8 9.0 %collective-permute-start.15 = (bf16[1,3,64,512]{3,2,1,0:T(8,128)(2,1)S(1)}, bf16[1,3,64,512]{3,2,1,0:T(8,128)(2,1)S(1)}, u32[]{:S(2)}, u32[]{:S(2)}) collective-permute-start(bf16[1,3,64,512]{3,2,1,0:T(8,128)(2,1)S(1)} %get-tuple-element.51.refs_0_), channel_id=1, source_target_pairs={{0,96},{16,112},{32,0},{48,16},{64,32},{80,48},{96,64},{112,80},{1... | collective-permute-start | bytes 589832 | tf_op jit(solution)/shard_map/ppermute | solution.py:393
  62.8 14.7 %collective-permute-start.18 = (bf16[1,3,64,512]{3,2,1,0:T(8,128)(2,1)S(1)}, bf16[1,3,64,512]{3,2,1,0:T(8,128)(2,1)S(1)}, u32[]{:S(2)}, u32[]{:S(2)}) collective-permute-start(bf16[1,3,64,512]{3,2,1,0:T(8,128)(2,1)S(1)} %get-tuple-element.51.refs_0_), channel_id=1, source_target_pairs={{0,16},{16,0},{32,48},{48,32},{64,80},{80,64},{96,112},{112,96},{1... | collective-permute-start | bytes 589832 | tf_op jit(solution)/shard_map/ppermute | solution.py:396
  66.4 11.1 %collective-permute-start.21 = (bf16[1,3,64,512]{3,2,1,0:T(8,128)(2,1)S(1)}, bf16[1,3,64,512]{3,2,1,0:T(8,128)(2,1)S(1)}, u32[]{:S(2)}, u32[]{:S(2)}) collective-permute-start(bf16[1,3,64,512]{3,2,1,0:T(8,128)(2,1)S(1)} %collective-permute-done.17.refs_3_), channel_id=1, source_target_pairs={{0,16},{16,0},{32,48},{48,32},{64,80},{80,64},{96,112},{112,96},{1... | collective-permute-start | bytes 589832 | tf_op jit(solution)/shard_map/ppermute | solution.py:396
  71.8 5.7 %collective-permute-start.20 = (bf16[1,3,64,512]{3,2,1,0:T(8,128)(2,1)S(1)}, bf16[1,3,64,512]{3,2,1,0:T(8,128)(2,1)S(1)}, u32[]{:S(2)}, u32[]{:S(2)}) collective-permute-start(bf16[1,3,64,512]{3,2,1,0:T(8,128)(2,1)S(1)} %collective-permute-done.16.refs_2_), channel_id=1, source_target_pairs={{0,16},{16,0},{32,48},{48,32},{64,80},{80,64},{96,112},{112,96},{1... | collective-permute-start | bytes 589832 | tf_op jit(solution)/shard_map/ppermute | solution.py:396
  71.8 5.7 %collective-permute-start.19 = (bf16[1,3,64,512]{3,2,1,0:T(8,128)(2,1)S(1)}, bf16[1,3,64,512]{3,2,1,0:T(8,128)(2,1)S(1)}, u32[]{:S(2)}, u32[]{:S(2)}) collective-permute-start(bf16[1,3,64,512]{3,2,1,0:T(8,128)(2,1)S(1)} %collective-permute-done.15.refs_1_), channel_id=1, source_target_pairs={{0,16},{16,0},{32,48},{48,32},{64,80},{80,64},{96,112},{112,96},{1... | collective-permute-start | bytes 589832 | tf_op jit(solution)/shard_map/ppermute | solution.py:396
  80.2 2.8 %collective-permute-start.22 = (bf16[3,256,512]{2,1,0:T(8,128)(2,1)S(1)}, bf16[3,256,512]{2,1,0:T(8,128)(2,1)S(1)}, u32[]{:S(2)}, u32[]{:S(2)}) collective-permute-start(bf16[3,256,512]{2,1,0:T(8,128)(2,1)S(1)} %shard_map.148), channel_id=1, source_target_pairs={{0,16},{16,0},{32,48},{48,32},{64,80},{80,64},{96,112},{112,96},{1... | collective-permute-start | bytes 2359304 | tf_op jit(solution)/shard_map/ppermute | solution.py:396
  83.2 9.5 %collective-permute-start.23 = (bf16[3,64,512]{2,1,0:T(8,128)(2,1)S(1)}, bf16[3,64,512]{2,1,0:T(8,128)(2,1)S(1)}, u32[]{:S(2)}, u32[]{:S(2)}) collective-permute-start(bf16[3,64,512]{2,1,0:T(8,128)(2,1)S(1)} %get-tuple-element.54), channel_id=1, source_target_pairs={{0,32},{16,48},{32,64},{48,80},{64,96},{80,112},{96,0},{112,16},{1... | collective-permute-start | bytes 589832 | tf_op jit(solution)/shard_map/ppermute | solution.py:393
  83.7 12.4 %collective-permute-start.24 = (bf16[3,64,512]{2,1,0:T(8,128)(2,1)S(1)}, bf16[3,64,512]{2,1,0:T(8,128)(2,1)S(1)}, u32[]{:S(2)}, u32[]{:S(2)}) collective-permute-start(bf16[3,64,512]{2,1,0:T(8,128)(2,1)S(1)} %get-tuple-element.55), channel_id=1, source_target_pairs={{0,64},{16,80},{32,96},{48,112},{64,0},{80,16},{96,32},{112,48},{1... | collective-permute-start | bytes 589832 | tf_op jit(solution)/shard_map/ppermute | solution.py:393
  86.9 9.7 %collective-permute-start.25 = (bf16[3,64,512]{2,1,0:T(8,128)(2,1)S(1)}, bf16[3,64,512]{2,1,0:T(8,128)(2,1)S(1)}, u32[]{:S(2)}, u32[]{:S(2)}) collective-permute-start(bf16[3,64,512]{2,1,0:T(8,128)(2,1)S(1)} %get-tuple-element.56), channel_id=1, source_target_pairs={{0,96},{16,112},{32,0},{48,16},{64,32},{80,48},{96,64},{112,80},{1... | collective-permute-start | bytes 589832 | tf_op jit(solution)/shard_map/ppermute | solution.py:393
  96.8 8.3 %collective-permute-start.28 = (bf16[200,512]{1,0:T(8,128)(2,1)S(1)}, bf16[200,512]{1,0:T(8,128)(2,1)S(1)}, u32[]{:S(2)}, u32[]{:S(2)}) collective-permute-start(bf16[200,512]{1,0:T(8,128)(2,1)S(1)} %shard_map.150.own_ref), channel_id=1, source_target_pairs={{0,3},{1,0},{2,1},{3,2},{4,7},{5,4},{6,5},{7,6},{8,11},{9,8},{10,9... | collective-permute-start | bytes 614408 | tf_op jit(solution)/shard_map/ppermute | solution.py:407
  99.6 7.4 %collective-permute-start.27 = (bf16[200,512]{1,0:T(8,128)(2,1)S(1)}, bf16[200,512]{1,0:T(8,128)(2,1)S(1)}, u32[]{:S(2)}, u32[]{:S(2)}) collective-permute-start(bf16[200,512]{1,0:T(8,128)(2,1)S(1)} %shard_map.150.own_ref), channel_id=1, source_target_pairs={{0,2},{1,3},{2,0},{3,1},{4,6},{5,7},{6,4},{7,5},{8,10},{9,11},{10,... | collective-permute-start | bytes 614408 | tf_op jit(solution)/shard_map/ppermute | solution.py:407
  100.4 8.7 %collective-permute-start.26 = (bf16[200,512]{1,0:T(8,128)(2,1)S(1)}, bf16[200,512]{1,0:T(8,128)(2,1)S(1)}, u32[]{:S(2)}, u32[]{:S(2)}) collective-permute-start(bf16[200,512]{1,0:T(8,128)(2,1)S(1)} %shard_map.150.own_ref), channel_id=1, source_target_pairs={{0,1},{1,2},{2,3},{3,0},{4,5},{5,6},{6,7},{7,4},{8,9},{9,10},{10,1... | collective-permute-start | bytes 614408 | tf_op jit(solution)/shard_map/ppermute | solution.py:407
  109.2 8.7 %collective-permute-start.31 = (bf16[200,512]{1,0:T(8,128)(2,1)S(1)}, bf16[200,512]{1,0:T(8,128)(2,1)S(1)}, u32[]{:S(2)}, u32[]{:S(2)}) collective-permute-start(bf16[200,512]{1,0:T(8,128)(2,1)S(1)} %shard_map.151.own_ref), channel_id=1, source_target_pairs={{0,12},{1,13},{2,14},{3,15},{4,0},{5,1},{6,2},{7,3},{8,4},{9,5},{1... | collective-permute-start | bytes 614408 | tf_op jit(solution)/shard_map/ppermute | solution.py:407
  112.3 7.4 %collective-permute-start.30 = (bf16[200,512]{1,0:T(8,128)(2,1)S(1)}, bf16[200,512]{1,0:T(8,128)(2,1)S(1)}, u32[]{:S(2)}, u32[]{:S(2)}) collective-permute-start(bf16[200,512]{1,0:T(8,128)(2,1)S(1)} %shard_map.151.own_ref), channel_id=1, source_target_pairs={{0,8},{1,9},{2,10},{3,11},{4,12},{5,13},{6,14},{7,15},{8,0},{9,1},... | collective-permute-start | bytes 614408 | tf_op jit(solution)/shard_map/ppermute | solution.py:407
  112.9 8.8 %collective-permute-start.29 = (bf16[200,512]{1,0:T(8,128)(2,1)S(1)}, bf16[200,512]{1,0:T(8,128)(2,1)S(1)}, u32[]{:S(2)}, u32[]{:S(2)}) collective-permute-start(bf16[200,512]{1,0:T(8,128)(2,1)S(1)} %shard_map.151.own_ref), channel_id=1, source_target_pairs={{0,4},{1,5},{2,6},{3,7},{4,8},{5,9},{6,10},{7,11},{8,12},{9,13},{1... | collective-permute-start | bytes 614408 | tf_op jit(solution)/shard_map/ppermute | solution.py:407
  (6 other events, 127.7 us)
